TPU v7x, 128 devices: a whole 4x4x4 slice. The times are simulated.
128 devices in a mesh: gx: 32 (over y, z, core), gy: 4 (over x).
Axes of the slice: x: 4, y: 4, z: 4, core: 2. Of those that a mesh axis runs over, the one named last changes fastest.
Arguments:
- vorticity_grid: float32 [4096, 4096], P(('gx', 'gy')), may hold values from -6 to 6
- forcing_grid: float32 [4096, 4096], P(('gx', 'gy')), may hold values from -12 to 12
- cutoff: int32 [1], replicated, may hold values from 853 to 1365
- forcing_shells: int32 [4], replicated, may hold values from 2 to 127
Outputs:
- lifted_spectrum: float32 [2, 4096, 4096], P(None, ('gx', 'gy'))
- coarse_field: float32 [256, 256], P(('gx', 'gy'))
Inputs may be any that keep to these rules, and one draw needn't show every extreme that they name: Nonlinear modes with an absolute wavenumber index above cutoff are removed.
All inputs are finite; a program needn't handle non-finite values.
Results may differ from a plain program's by a relative error of at most 0.0001.
Values sent between devices are 32-bit elements; how exact they have to be, the bound alone decides.
No kernel may reach another device: no remote copies, remote signals or barrier semaphores. Data moves between devices by JAX's collectives and lax.ppermute only.
A program may use at most 128 MiB of HBM per device.

v0:
```python
import math

import jax
import jax.numpy as jnp
from jax import lax
from jax.sharding import PartitionSpec as P

RADIX = 64
LOW = 256
SHELLS = 4


time_step = 0.05
viscosity = 0.05
coarse_ratio = 4.0


def signed_index(index_array, length_of):
    return jnp.where(index_array < length_of // 2, index_array, index_array - length_of)


def pair_tables(first_ids, second_ids, length_of):
    product = first_ids[:, None] * second_ids[None, :] % length_of
    phases = 2.0 * math.pi / length_of * product.astype(jnp.float32)
    factor = 1.0 / math.sqrt(length_of)
    return (jnp.cos(phases) * factor, jnp.sin(phases) * factor)


def contract(pattern, left_side, right_side):
    return jnp.einsum(pattern, left_side, right_side, precision=lax.Precision.HIGHEST)


def complex_table(direction):
    indices = jnp.arange(RADIX, dtype=jnp.int32)
    cos_table, sin_table = pair_tables(indices, indices, RADIX)
    signed_sin = direction * sin_table
    from_real = jnp.stack([cos_table, signed_sin], axis=1)
    from_imag = jnp.stack([-signed_sin, cos_table], axis=1)
    return jnp.stack([from_real, from_imag], axis=0)


def dft_last(values, direction, is_real):
    length_of = values.shape[-1]
    table = complex_table(direction)
    if is_real:
        leading = values.shape[:-1]
        split_values = values.reshape(leading + (RADIX, RADIX))
        first = contract("...ab,adk->d...kb", split_values, table[0])
    else:
        leading = values.shape[1:-1]
        split_values = values.reshape((2,) + leading + (RADIX, RADIX))
        first = contract("c...ab,cadk->d...kb", split_values, table)
    indices = jnp.arange(RADIX, dtype=jnp.int32)
    twiddle_index = indices[:, None] * indices[None, :] % length_of
    twiddle_phase = 2.0 * math.pi / length_of * twiddle_index.astype(jnp.float32)
    twiddle_real = jnp.cos(twiddle_phase)
    twiddle_imag = direction * jnp.sin(twiddle_phase)
    turned = jnp.stack(
        [
            first[0] * twiddle_real - first[1] * twiddle_imag,
            first[0] * twiddle_imag + first[1] * twiddle_real,
        ]
    )
    final = contract("c...kb,cbdj->d...jk", turned, table)
    return final.reshape((2,) + leading + (length_of,))


def rows_to_grid(packed):
    return lax.all_to_all(packed, ("gx", "gy"), split_axis=1, concat_axis=2, tiled=True)


def rows_to_waves(packed):
    return lax.all_to_all(packed, ("gx", "gy"), split_axis=2, concat_axis=1, tiled=True)


def forward(fields):
    field_count = fields.shape[0]
    half = dft_last(fields, -1.0, True)
    moved = rows_to_waves(half.reshape((2 * field_count,) + half.shape[2:]))
    moved = jnp.swapaxes(moved, 1, 2)
    return dft_last(moved.reshape((2, field_count) + moved.shape[1:]), -1.0, False)


def inverse(spectra):
    field_count = spectra.shape[1]
    half = dft_last(spectra, 1.0, False)
    packed = jnp.swapaxes(half.reshape((2 * field_count,) + half.shape[2:]), 1, 2)
    moved = rows_to_grid(packed)
    return dft_last(moved.reshape((2, field_count) + moved.shape[1:]), 1.0, False)


def body(vorticity_grid, forcing_grid, cutoff, forcing_shells):
    row_count = vorticity_grid.shape[0]
    grid_size = vorticity_grid.shape[1]
    device_rank = lax.axis_index("gx") * lax.axis_size("gy") + lax.axis_index("gy")
    device_total = lax.axis_size("gx") * lax.axis_size("gy")
    row_start = device_rank * row_count
    row_ids = row_start + jnp.arange(row_count, dtype=jnp.int32)
    col_ids = jnp.arange(grid_size, dtype=jnp.int32)
    wave_y = signed_index(row_ids, grid_size)[:, None]
    wave_x = signed_index(col_ids, grid_size)[None, :]
    wave_unit = 2.0 * math.pi / grid_size
    deriv_y = (
        jnp.where(row_ids[:, None] == grid_size // 2, 0, wave_y).astype(jnp.float32) * wave_unit
    )
    deriv_x = (
        jnp.where(col_ids[None, :] == grid_size // 2, 0, wave_x).astype(jnp.float32) * wave_unit
    )
    squares = wave_x * wave_x + wave_y * wave_y
    laplace = squares.astype(jnp.float32) * (wave_unit * wave_unit)
    inverse_lap = jnp.where(squares == 0, 0.0, 1.0 / jnp.maximum(laplace, wave_unit * wave_unit))
    dealias = (jnp.abs(wave_x) <= cutoff[0]) & (jnp.abs(wave_y) <= cutoff[0])
    shell_mask = jnp.zeros((row_count, grid_size), dtype=bool)
    for shell_index in range(SHELLS):
        radius = forcing_shells[shell_index]
        shell_mask = shell_mask | (radius * radius <= squares) & (
            squares < (radius + 1) * (radius + 1)
        )
    started = forward(jnp.stack([vorticity_grid, forcing_grid]))
    drive_real = jnp.where(shell_mask, started[0, 1], 0.0)
    drive_imag = jnp.where(shell_mask, started[1, 1], 0.0)
    state_real = started[0, 0]
    state_imag = started[1, 0]

    def tendency(now_real, now_imag):
        stream_real = now_real * inverse_lap
        stream_imag = now_imag * inverse_lap
        speed_real = deriv_x * stream_real - deriv_y * stream_imag
        speed_imag = deriv_x * stream_imag + deriv_y * stream_real
        slope_real = -deriv_y * now_real - deriv_x * now_imag
        slope_imag = -deriv_y * now_imag + deriv_x * now_real
        spectra = jnp.stack(
            [jnp.stack([speed_real, slope_real]), jnp.stack([speed_imag, slope_imag])]
        )
        grids = inverse(spectra)
        advect = grids[0, 0] * grids[0, 1] + grids[1, 0] * grids[1, 1]
        term = forward(advect[None])
        out_real = (
            -jnp.where(dealias, term[0, 0], 0.0) - viscosity * laplace * now_real + drive_real
        )
        out_imag = (
            -jnp.where(dealias, term[1, 0], 0.0) - viscosity * laplace * now_imag + drive_imag
        )
        return (out_real, out_imag)

    earlier_real = state_real
    earlier_imag = state_imag
    first_real, first_imag = tendency(state_real, state_imag)
    second_real, second_imag = tendency(
        state_real + time_step * first_real, state_imag + time_step * first_imag
    )
    state_real = state_real + 0.5 * time_step * (first_real + second_real)
    state_imag = state_imag + 0.5 * time_step * (first_imag + second_imag)
    projected_real = state_real + coarse_ratio * (state_real - earlier_real)
    projected_imag = state_imag + coarse_ratio * (state_imag - earlier_imag)
    half_low = LOW // 2
    low_modes = (
        (wave_x >= -half_low) & (wave_x < half_low) & (wave_y >= -half_low) & (wave_y < half_low)
    )
    lifted_real = jnp.where(low_modes, projected_real, state_real)
    lifted_imag = jnp.where(low_modes, projected_imag, state_imag)
    projected = jnp.stack([projected_real, projected_imag])
    low_columns = jnp.concatenate(
        [projected[:, :, :half_low], projected[:, :, grid_size - half_low :]], axis=2
    )
    block_ids = jnp.arange(LOW, dtype=jnp.int32)
    coarse_rows = LOW // device_total
    every_row = lax.all_gather(low_columns, ("gx", "gy"), axis=1, tiled=True)
    block_low = jnp.concatenate(
        [every_row[:, :half_low], every_row[:, grid_size - half_low :]], axis=1
    )
    own_ids = device_rank * coarse_rows + jnp.arange(coarse_rows, dtype=jnp.int32)
    column_cos, column_sin = pair_tables(block_ids, own_ids, LOW)
    mixed_real = contract("qp,pa->qa", block_low[0], column_cos) - contract(
        "qp,pa->qa", block_low[1], column_sin
    )
    mixed_imag = contract("qp,pa->qa", block_low[0], column_sin) + contract(
        "qp,pa->qa", block_low[1], column_cos
    )
    row_cos, row_sin = pair_tables(block_ids, block_ids, LOW)
    coarse = contract("qa,qb->ab", mixed_real, row_cos) - contract("qa,qb->ab", mixed_imag, row_sin)
    return (jnp.stack([lifted_real, lifted_imag]), coarse)


def solution(mesh):
    placed = (P(("gx", "gy"), None), P(("gx", "gy"), None), P(), P())
    return jax.shard_map(
        body,
        mesh=mesh,
        in_specs=placed,
        out_specs=(P(None, ("gx", "gy"), None), P(("gx", "gy"), None)),
        check_vma=False,
    )
```

profile of v0, /device:TPU:1, one launch (start us, length us, event | category | flops | bytes accessed | tf_op | source)
XLA Modules:
  0.0 652.1 jit_solution(10247659187986664976)
XLA Ops:
  14.8 7.7 %fusion.41 = f32[2,2,32,64,64]{4,3,2,1,0:T(8,128)} fusion(f32[2,64,2,64,1,1]{1,3,2,0,5,4:T(8,128)S(1)} %get-tuple-element.52, f32[1,2,32,64,64]{4,3,2,1,0:T(8,128)S(1)} %get-tuple-element.22, f32[1,2,32,64,64]{4,3,2,1,0:T(8,128)S(1)} %get-tuple-element.21), kind=kOutput, calls=%fused_computation.73 | convolution fusion | flops 805830656 | bytes 4259840 | tf_op jit(solution)/shard_map/c...kb,cbdj->d...jk/dot_general | solution.py:30
  22.5 12.3 %copy.164 = f32[2,2,32,64,64]{2,1,0,4,3:T(2,128)} copy(f32[2,2,32,64,64]{4,3,2,1,0:T(8,128)} %fusion.41) | data formatting | bytes 4194304 | tf_op jit(solution)/shard_map/reshape;reshape | solution.py:79
  34.8 8.7 %reshape.2032 = f32[128,1,4096]{2,1,0:T(1,128)} reshape(f32[4096,4,32]{2,1,0:T(4,128)} %bitcast.418) | data formatting | bytes 4194304
  43.5 11.8 %all-to-all-start = ((f32[128,1,4096]{2,1,0:T(1,128)}), f32[128,1,4096]{2,1,0:T(1,128)S(1)}, u32[]{:S(2)}, u32[]{:S(2)}) async-start(f32[128,1,4096]{2,1,0:T(1,128)} %reshape.2032), calls=%async_computation | async-start | bytes 4194304 | tf_op jit(solution)/shard_map/all_to_all | solution.py:73
  56.7 29.4 %all-to-all-done = f32[128,1,4096]{2,1,0:T(1,128)S(1)} async-done(((f32[128,1,4096]{2,1,0:T(1,128)}), f32[128,1,4096]{2,1,0:T(1,128)S(1)}, u32[]{:S(2)}, u32[]{:S(2)}) %all-to-all-start) | async-done | bytes 2097184 | tf_op jit(solution)/shard_map/all_to_all | solution.py:73
  88.0 7.3 %reduce = f32[128,4096]{1,0:T(8,128)S(1)} reduce(f32[128,1,4096]{2,1,0:T(1,128)} %copy-done.2, f32[]{:T(128)} %broadcast.2187), dimensions={1}, to_apply=%all_to_all.61.reduce_sub_computation | reduce | bytes 4194308 | tf_op jit(solution)/shard_map/all_to_all | solution.py:73
  101.3 11.5 %copy.327 = f32[4,32,128,32]{1,2,3,0:T(8,128)} copy(f32[4,32,128,32]{1,0,3,2:T(4,128)} %bitcast.421) | data formatting | bytes 4194304 | tf_op jit(solution)/shard_map/all_to_all | solution.py:73
  128.9 7.7 %fusion.47 = f32[2,2,32,64,64]{4,3,2,1,0:T(8,128)} fusion(f32[2,64,2,64,1,1]{1,3,2,0,5,4:T(8,128)S(1)} %get-tuple-element.52, f32[1,2,32,64,64]{4,3,2,1,0:T(8,128)S(1)} %get-tuple-element.20, f32[1,2,32,64,64]{4,3,2,1,0:T(8,128)S(1)} %get-tuple-element.19), kind=kOutput, calls=%fused_computation.75 | convolution fusion | flops 805830656 | bytes 4259840 | tf_op jit(solution)/shard_map/c...kb,cbdj->d...jk/dot_general | solution.py:30
  152.6 7.7 %fusion.50 = f32[2,2,32,64,64]{4,3,2,1,0:T(8,128)} fusion(f32[1,2,32,64,64]{4,3,2,1,0:T(8,128)S(1)} %get-tuple-element.18, f32[1,2,32,64,64]{4,3,2,1,0:T(8,128)S(1)} %get-tuple-element.17, f32[1,64,2,64]{1,3,2,0:T(8,128)S(1)} %get-tuple-element.54, f32[1,64,2,64]{1,3,2,0:T(8,128)S(1)} %get-tuple-element.53), kind=kOutput, calls=%fused_computation.76 | convolution fusion | flops 805847040 | bytes 4259840 | tf_op jit(solution)/shard_map/c...kb,cbdj->d...jk/dot_general | solution.py:30
  160.3 12.3 %copy.179 = f32[2,2,32,64,64]{2,1,0,4,3:T(2,128)} copy(f32[2,2,32,64,64]{4,3,2,1,0:T(8,128)} %fusion.50) | data formatting | bytes 4194304 | tf_op jit(solution)/shard_map/reshape;reshape | solution.py:87
  172.6 8.7 %reshape.2034 = f32[128,1,4096]{2,1,0:T(1,128)} reshape(f32[4096,4,32]{2,1,0:T(4,128)} %bitcast.419) | data formatting | bytes 4194304
  181.3 35.8 %all_to_all.84 = f32[128,1,4096]{2,1,0:T(1,128)} all-to-all(f32[128,1,4096]{2,1,0:T(1,128)} %reshape.2034), channel_id=1, replica_groups=mesh['gx'=32,'gy'=4] {'gx','gy'}, dimensions={0} | all-to-all | bytes 4194304 | tf_op jit(solution)/shard_map/all_to_all | solution.py:69
  217.1 8.7 %reduce.1 = f32[128,4096]{1,0:T(8,128)} reduce(f32[128,1,4096]{2,1,0:T(1,128)} %all_to_all.84, f32[]{:T(128)} %broadcast.2187), dimensions={1}, to_apply=%all_to_all.65.reduce_sub_computation | reduce | bytes 4194308 | tf_op jit(solution)/shard_map/all_to_all | solution.py:69
  225.8 7.4 %reshape.2035 = f32[4096,4,32]{2,1,0:T(4,128)} reshape(f32[128,4096]{1,0:T(8,128)} %reduce.1) | data formatting | bytes 4194304
  233.2 11.5 %copy.326 = f32[4,128,32,32]{3,1,2,0:T(8,128)} copy(f32[4,128,32,32]{3,0,2,1:T(4,128)} %bitcast.423) | data formatting | bytes 4194304 | tf_op jit(solution)/shard_map/all_to_all | solution.py:69
  244.7 7.7 %reshape_reshape.29 = f32[2,2,32,64,64]{4,3,2,1,0:T(8,128)} reshape(f32[4,32,128,32]{3,2,1,0:T(8,128)} %bitcast.425) | data formatting | bytes 4194304 | tf_op jit(solution)/shard_map/reshape;reshape | solution.py:51
  258.9 7.7 %fusion.56 = f32[2,2,32,64,64]{4,3,2,1,0:T(8,128)} fusion(f32[1,2,32,64,64]{4,3,2,1,0:T(8,128)S(1)} %get-tuple-element.16, f32[1,2,32,64,64]{4,3,2,1,0:T(8,128)S(1)} %get-tuple-element.15, f32[1,64,2,64]{1,3,2,0:T(8,128)S(1)} %get-tuple-element.54, f32[1,64,2,64]{1,3,2,0:T(8,128)S(1)} %get-tuple-element.53), kind=kOutput, calls=%fused_computation.78 | convolution fusion | flops 805847040 | bytes 4259840 | tf_op jit(solution)/shard_map/c...kb,cbdj->d...jk/dot_general | solution.py:30
  284.2 6.7 %copy.182 = f32[2,1,32,64,64]{2,0,4,3,1:T(2,128)} copy(f32[2,1,32,64,64]{4,3,2,0,1:T(8,128)} %fusion.83) | data formatting | bytes 2097152 | tf_op jit(solution)/shard_map/reshape;reshape | solution.py:79
  290.9 6.7 %reshape.2036 = f32[128,1,2048]{2,1,0:T(1,128)} reshape(f32[4096,2,32]{2,1,0:T(2,128)} %bitcast.427) | data formatting | bytes 2097152
  333.1 6.7 %copy.329 = f32[2,32,128,32]{1,2,3,0:T(8,128)} copy(f32[2,32,128,32]{1,0,3,2:T(2,128)} %bitcast.429) | data formatting | bytes 2097152 | tf_op jit(solution)/shard_map/all_to_all | solution.py:73
  365.7 7.7 %fusion.59 = f32[2,2,32,64,64]{4,3,2,1,0:T(8,128)} fusion(f32[1,2,32,64,64]{4,3,2,1,0:T(8,128)S(1)} %get-tuple-element.14, f32[1,2,32,64,64]{4,3,2,1,0:T(8,128)S(1)} %get-tuple-element.13, f32[1,64,2,64]{1,3,2,0:T(8,128)S(1)} %get-tuple-element.54, f32[1,64,2,64]{1,3,2,0:T(8,128)S(1)} %get-tuple-element.53), kind=kOutput, calls=%fused_computation.79 | convolution fusion | flops 805847040 | bytes 4259840 | tf_op jit(solution)/shard_map/c...kb,cbdj->d...jk/dot_general | solution.py:30
  373.4 12.3 %copy.202 = f32[2,2,32,64,64]{2,1,0,4,3:T(2,128)} copy(f32[2,2,32,64,64]{4,3,2,1,0:T(8,128)} %fusion.59) | data formatting | bytes 4194304 | tf_op jit(solution)/shard_map/reshape;reshape | solution.py:87
  385.7 8.7 %reshape.2038 = f32[128,1,4096]{2,1,0:T(1,128)} reshape(f32[4096,4,32]{2,1,0:T(4,128)} %bitcast.420) | data formatting | bytes 4194304
  394.3 36.0 %all_to_all.85 = f32[128,1,4096]{2,1,0:T(1,128)} all-to-all(f32[128,1,4096]{2,1,0:T(1,128)} %reshape.2038), channel_id=1, replica_groups=mesh['gx'=32,'gy'=4] {'gx','gy'}, dimensions={0} | all-to-all | bytes 4194304 | tf_op jit(solution)/shard_map/all_to_all | solution.py:69
  430.4 8.7 %reduce.3 = f32[128,4096]{1,0:T(8,128)} reduce(f32[128,1,4096]{2,1,0:T(1,128)} %all_to_all.85, f32[]{:T(128)} %broadcast.2187), dimensions={1}, to_apply=%all_to_all.72.reduce_sub_computation | reduce | bytes 4194308 | tf_op jit(solution)/shard_map/all_to_all | solution.py:69
  439.0 7.4 %reshape.2039 = f32[4096,4,32]{2,1,0:T(4,128)} reshape(f32[128,4096]{1,0:T(8,128)} %reduce.3) | data formatting | bytes 4194304
  446.5 11.5 %copy.325 = f32[4,128,32,32]{3,1,2,0:T(8,128)} copy(f32[4,128,32,32]{3,0,2,1:T(4,128)} %bitcast.424) | data formatting | bytes 4194304 | tf_op jit(solution)/shard_map/all_to_all | solution.py:69
  458.0 7.6 %reshape_reshape.32 = f32[2,2,32,64,64]{4,3,2,1,0:T(8,128)} reshape(f32[4,32,128,32]{3,2,1,0:T(8,128)} %bitcast.426) | data formatting | bytes 4194304 | tf_op jit(solution)/shard_map/reshape;reshape | solution.py:51
  472.1 7.7 %fusion.65 = f32[2,2,32,64,64]{4,3,2,1,0:T(8,128)} fusion(f32[1,2,32,64,64]{4,3,2,1,0:T(8,128)S(1)} %get-tuple-element.12, f32[1,2,32,64,64]{4,3,2,1,0:T(8,128)S(1)} %get-tuple-element.11, f32[1,64,2,64]{1,3,2,0:T(8,128)S(1)} %get-tuple-element.54, f32[1,64,2,64]{1,3,2,0:T(8,128)S(1)} %get-tuple-element.53), kind=kOutput, calls=%fused_computation.81 | convolution fusion | flops 805847040 | bytes 4259840 | tf_op jit(solution)/shard_map/c...kb,cbdj->d...jk/dot_general | solution.py:30
  495.1 6.7 %copy.205 = f32[2,1,32,64,64]{2,0,4,3,1:T(2,128)} copy(f32[2,1,32,64,64]{4,3,2,0,1:T(8,128)} %fusion.89) | data formatting | bytes 2097152 | tf_op jit(solution)/shard_map/reshape;reshape | solution.py:79
  519.5 13.1 %all-to-all-done.4 = f32[128,1,2048]{2,1,0:T(1,128)} async-done(((f32[128,1,2048]{2,1,0:T(1,128)}), f32[128,1,2048]{2,1,0:T(1,128)}, u32[]{:S(2)}, u32[]{:S(2)}) %all-to-all-start.4) | async-done | bytes 1048608 | tf_op jit(solution)/shard_map/all_to_all | solution.py:73
  573.6 63.9 %all-gather.2.cloned.1.call-done = f32[2,4096,256]{2,1,0:T(8,128)} async-done(((f32[2,32,256]{2,1,0:T(8,128)}), f32[2,4096,256]{2,1,0:T(8,128)}) %all-gather.2.cloned.1.call-update) | async-done | bytes 8388624 | tf_op jit(solution)/shard_map/all_gather | solution.py:168
  (137 shorter events, 213.7 us)
Async XLA Ops:
  7.2 2.1 copy-start.11
  7.3 3.1 copy-start.7
  43.5 42.7 %all-to-all-start = ((f32[128,1,4096]{2,1,0:T(1,128)}), f32[128,1,4096]{2,1,0:T(1,128)S(1)}, u32[]{:S(2)}, u32[]{:S(2)}) async-start(f32[128,1,4096]{2,1,0:T(1,128)} %reshape.2032), calls=%async_computation | async-start | bytes 4194304 | tf_op jit(solution)/shard_map/all_to_all | solution.py:73
  55.3 90.3 %copy-start.14 = (f32[32]{0:T(128)}, f32[32]{0:T(128)S(1)}, u32[]{:S(2)}) copy-start(f32[32]{0:T(128)S(1)} %get-tuple-element.67) | copy-start | bytes 388
  55.3 90.3 %copy-start.16 = (f32[32]{0:T(128)}, f32[32]{0:T(128)S(1)}, u32[]{:S(2)}) copy-start(f32[32]{0:T(128)S(1)} %get-tuple-element.68) | copy-start | bytes 388
  86.1 1.4 copy-start.2
  297.6 4.8 copy-start.13
  297.6 24.3 %all-to-all-start.2 = ((f32[128,1,2048]{2,1,0:T(1,128)}), f32[128,1,2048]{2,1,0:T(1,128)}, u32[]{:S(2)}, u32[]{:S(2)}) async-start(f32[128,1,2048]{2,1,0:T(1,128)} %reshape.2036), calls=%async_computation.2 | async-start | bytes 2097152 | tf_op jit(solution)/shard_map/all_to_all | solution.py:73
  354.3 0.9 copy-start.12
  355.2 3.2 copy-start.1
  355.2 3.2 copy-start.3
  355.2 3.2 copy-start.4
  355.2 3.2 copy-start.9
  355.2 3.2 copy-start.10
  355.2 3.2 copy-start.15
  358.3 1.8 copy-start
  358.4 1.7 copy-start.17
  484.6 3.9 copy-start.8
  508.4 24.1 %all-to-all-start.4 = ((f32[128,1,2048]{2,1,0:T(1,128)}), f32[128,1,2048]{2,1,0:T(1,128)}, u32[]{:S(2)}, u32[]{:S(2)}) async-start(f32[128,1,2048]{2,1,0:T(1,128)} %reshape.2040), calls=%async_computation.4 | async-start | bytes 2097152 | tf_op jit(solution)/shard_map/all_to_all | solution.py:73
  513.1 124.4 %all-gather.2.cloned.1.call-start = ((), (), s32[]{:S(2)}) async-start(), calls=%async_computation.5 | async-start | bytes 8454144 | tf_op jit(solution)/shard_map/all_gather | solution.py:168
  568.9 2.0 copy-start.5
  568.9 2.0 copy-start.6
  570.9 1.4 copy-start.18
Sparse Core Ops, SparseCore 0:
  572.3 65.0 all-gather.1
where the time goes:
time: 663 us; the launch traced here: 652 us
  local copies, waits for them, and re-layouts  258 us (39%)
  waiting for transfers between devices  111 us (17%)
  matrix products  107 us (16%)
  blocking collectives  71.8 us (11%)
  other arithmetic  58.8 us (9%)
  between operations  23.3 us (4%)
  starting transfers between devices  21.4 us (3%)
    dot_general x26, matrix products, contract(): jnp.einsum(pattern, left_side, right_side, precision=lax.Precision.HIGHEST)  107 us
    unnamed x48, local copies, waits for them, and re-layouts  73.1 us
    all_to_all x2, blocking collectives, rows_to_grid(): lax.all_to_all(packed, ('gx', 'gy'), split_axis=1, concat_axis=2, tiled=T...  71.8 us
    all_gather x1, waiting for transfers between devices, body(): every_row = lax.all_gather(low_columns, ('gx', 'gy'), axis=1, tiled=True)  63.9 us
    all_to_all x3, waiting for transfers between devices, rows_to_waves(): lax.all_to_all(packed, ('gx', 'gy'), split_axis=2, concat_axis=1, tiled=T...  47.5 us
    all_to_all x7, local copies, waits for them, and re-layouts, rows_to_waves(): lax.all_to_all(packed, ('gx', 'gy'), split_axis=2, concat_axis=1, tiled=T...  39.8 us
    another operation x3, local copies, waits for them, and re-layouts, forward(): moved = rows_to_waves(half.reshape((2 * field_count,) + half.shape[2:]))  25.7 us
    another operation x2, local copies, waits for them, and re-layouts, inverse(): half.reshape((2 * field_count,) + half.shape[2:])  24.6 us
  transfers between devices with their start and end apart: 4, of which 4 were waited for; matrix products, arithmetic and copies ran while one was open for 2% of the time, Pallas kernels for 0%

commit v1 on v0

v1 whole, which is shorter than its diff:
```python
import functools
import math

import jax
import jax.numpy as jnp
import numpy as np
from jax import lax
from jax.experimental import pallas as pl
from jax.experimental.pallas import tpu as pltpu
from jax.sharding import PartitionSpec as P

GRID = 4096
LANES = 128
LOW = 256
SHELLS = 4
VMEM_LIMIT = 24
AXES = ("gx", "gy")

time_step = 0.05
viscosity = 0.05
coarse_ratio = 4.0
unit = 2.0 * math.pi / GRID


def split_np(table, axis):
    high = table.astype(np.float32).astype(jnp.bfloat16)
    low = (table - high.astype(np.float64)).astype(np.float32).astype(jnp.bfloat16)
    return np.concatenate([high, low], axis=axis)


@functools.lru_cache(None)
def tables():
    made = {}
    index = np.arange(128)
    rows = index[:, None]
    angle = 2 * np.pi * np.outer(index, index) / 128
    cos, sin = np.cos(angle) / 8, np.sin(angle) / 8
    made["left"] = split_np(np.block([[cos, sin], [-sin, cos]]), 1)

    lane = np.arange(128)
    inner = 8 * (lane >> 5) + (lane & 7)
    slot = (lane >> 3) & 3
    same = slot[:, None] == slot[None, :]
    angle = 2 * np.pi * np.outer(inner, inner) / 32
    cos, sin = same * np.cos(angle) / 8, same * np.sin(angle) / 8
    made["right_x"] = split_np(np.block([[cos, -sin], [sin, cos]]), 0)

    wide = np.arange(256)
    col_j, col_x = wide >> 3, wide & 7
    out_t, out_x = lane >> 3, lane & 7
    same = col_x[:, None] == out_x[None, :]
    angle = 2 * np.pi * np.outer(col_j, out_t) / 32
    part0 = np.cos(angle)
    part1 = -np.sin(angle)
    part1[:, out_t == 0] = np.where(col_j % 2 == 0, 1.0, -1.0)[:, None]
    right_y = np.concatenate([same * part0, same * part1], axis=1) / 8
    made["forward_y"] = split_np(right_y, 0)
    made["inverse_y"] = split_np(right_y.T, 0)

    turn = 2 * np.pi * rows * inner[None, :] / GRID
    made["turn_x"] = planes([np.cos(turn), np.sin(turn)])
    turn_d = 2 * np.pi * rows * out_t[None, :] / GRID
    back = np.where(out_t == 0, 16, 32 - out_t)
    turn_m = 2 * np.pi * rows * back[None, :] / GRID
    made["turn_y"] = planes([np.cos(turn_d), np.sin(turn_d), np.cos(turn_m), np.sin(turn_m)])
    half = 2 * np.pi * rows / 256 + np.zeros((128, 128))
    made["half"] = planes([np.cos(half), np.sin(half)])

    angle = 2 * np.pi * np.outer(index, index) / GRID
    low = np.concatenate([np.cos(angle), -np.sin(angle)], axis=0) / 64
    made["low_rows"] = split_np(low, 1)
    turn = 2 * np.pi * rows * out_t[None, :] / 32
    made["turn_low"] = planes([np.cos(turn), np.sin(turn)])

    grid = np.arange(512)
    t, group, part, source = grid >> 5, (grid >> 4) & 1, (grid >> 3) & 1, grid & 7
    number = np.where(group == 0, t, np.where(t == 0, 16, 32 - t))
    wave = 32 * source + number
    point = np.arange(LOW)[None, :]
    angle = 2 * np.pi * (wave[:, None] * point % LOW) / LOW
    weight = np.where(wave == 0, 1.0, np.where(wave < 128, 2.0, 0.0))
    weight = np.where((wave == 128) & (part == 0), 1.0, weight)
    value = np.where(part[:, None] == 0, np.cos(angle), -np.sin(angle))
    made["coarse_y"] = split_np(weight[:, None] * value, 0)
    away = np.arange(128)[:, None]
    own = np.arange(32)[None, :]
    parts = []
    for odd in range(2):
        place = 32 * away + 16 * odd - own
        kernel = 1.0 + 2.0 * sum(
            np.cos(2 * np.pi * (p * place % GRID) / GRID) for p in range(1, 128)
        )
        sign = 1.0 - 2.0 * odd
        edge = 2 * np.pi * own / 32 + 0 * away
        parts.append(
            np.concatenate([kernel + sign * np.cos(edge), sign * np.sin(edge)], axis=1)
        )
    scale = -(1 + coarse_ratio) * 0.5 * time_step / (64 * LOW)
    both = np.concatenate(parts, axis=0) * scale
    both = split_np(both, 1)
    high, low = both[:, :64], both[:, 64:]
    made["coarse_x"] = np.concatenate([high, high, low, 0 * low], axis=1)
    return made


def planes(parts):
    return np.concatenate(parts, axis=0).astype(np.float32)


def halves(values):
    high = values.astype(jnp.bfloat16)
    low = (values - high.astype(jnp.float32)).astype(jnp.bfloat16)
    return high, low


def dot(left_side, right_side):
    return jnp.dot(left_side, right_side, preferred_element_type=jnp.float32)


def thrice(table, axis):
    size = table.shape[axis] // 2
    high = lax.slice_in_dim(table, 0, size, axis=axis)
    low = lax.slice_in_dim(table, size, 2 * size, axis=axis)
    return jnp.concatenate([high, high, low], axis=axis)


def left_many(left_table, real, imag):
    count = len(real)
    stacked = jnp.concatenate(
        [jnp.concatenate(real, axis=1), jnp.concatenate(imag, axis=1)], axis=0
    )
    high, low = halves(stacked)
    out = dot(thrice(left_table, 1), jnp.concatenate([high, low, high], axis=0))
    cut = lambda row, place: out[row : row + 128, 128 * place : 128 * place + 128]
    return [cut(0, k) for k in range(count)], [cut(128, k) for k in range(count)]


def right_many(right_table, first, second):
    count = len(first)
    stacked = jnp.concatenate(
        [jnp.concatenate([a, b], axis=1) for a, b in zip(first, second)], axis=0
    )
    high, low = halves(stacked)
    out = dot(jnp.concatenate([high, low, high], axis=1), thrice(right_table, 0))
    cut = lambda row, col: out[128 * row : 128 * row + 128, col : col + 128]
    return [cut(k, 0) for k in range(count)], [cut(k, 128) for k in range(count)]


def lane_ids():
    return lax.broadcasted_iota(jnp.int32, (128, 128), 1)


def row_ids():
    return lax.broadcasted_iota(jnp.int32, (128, 128), 0)


def roll(block, shift):
    shift = shift % 128
    return block if shift == 0 else pltpu.roll(block, shift, 1)


def swap4(blocks):
    lane = lax.broadcasted_iota(jnp.int32, blocks[0].shape, 1)
    out = list(blocks)
    for bit, shift in ((0, 32), (1, 64)):
        low = ((lane >> (5 + bit)) & 1) == 0
        made = list(out)
        for index in range(4):
            if (index >> bit) & 1 == 0:
                a, b = out[index], out[index | (1 << bit)]
                made[index] = jnp.where(low, a, roll(b, shift))
                made[index | (1 << bit)] = jnp.where(low, roll(a, -shift), b)
        out = made
    return out


def turned(real, imag, cos, sin):
    return real * cos + imag * sin, imag * cos - real * sin


class Tables:
    def __init__(self, names, refs):
        self.refs = dict(zip(names, refs))

    def __getitem__(self, name):
        return self.refs[name][...]

    def turn(self, name, index):
        return self.refs[name][128 * index : 128 * index + 128, :]


def x_turned(tab, first, second):
    cos, sin = tab.turn("turn_x", 0), tab.turn("turn_x", 1)
    pairs = [turned(a, b, cos, sin) for a, b in zip(first, second)]
    return [p[0] for p in pairs], [p[1] for p in pairs]


def x_plain(tab, real, imag):
    real, imag = left_many(tab["left"], real, imag)
    return right_many(tab["right_x"], *x_turned(tab, real, imag))


def x_forward(tab, real, imag):
    return x_plain(tab, swap4(real), swap4(imag))


def x_inverse(tab, real, imag):
    first, second = right_many(tab["right_x"], imag, real)
    first, second = left_many(tab["left"], *x_turned(tab, first, second))
    return second, first


def y_forward(tab, groups):
    part0, part1 = right_many(
        tab["forward_y"], [g[0] for g in groups], [g[1] for g in groups]
    )
    start = lane_ids() < 8
    cos, sin = tab.turn("turn_y", 0), tab.turn("turn_y", 1)
    rest = jnp.where(start, 0.0, cos)
    real = [p * cos + q * sin for p, q in zip(part0, part1)]
    imag = [q * rest - p * sin for p, q in zip(part0, part1)]
    direct = left_many(tab["left"], real, imag)
    cos, sin = tab.turn("turn_y", 2), tab.turn("turn_y", 3)
    a, b = jnp.where(start, 0.0, cos), jnp.where(start, cos, -sin)
    d, e = jnp.where(start, 0.0, -sin), jnp.where(start, -sin, -cos)
    real = [p * a + q * b for p, q in zip(part0, part1)]
    imag = [p * d + q * e for p, q in zip(part0, part1)]
    mirror = left_many(tab["left"], real, imag)
    return direct, mirror


def y_inverse(tab, real, imag, last, place):
    imag, real = left_many(tab["left"], imag, real)
    start = lane_ids() < 8
    cos, sin = tab.turn("turn_y", 0), tab.turn("turn_y", 1)
    cos = jnp.where(start, cos, 2.0 * cos)
    sin = 2.0 * sin
    part0 = [p * cos - q * sin for p, q in zip(real, imag)]
    part1 = [p * sin + q * cos for p, q in zip(real, imag)]
    part1 = [
        jnp.where(start, roll(last, -(32 * xh + 8 * place)), part1[xh]) for xh in range(4)
    ]
    return right_many(tab["inverse_y"], part0, part1)


def last_row(tab, real, imag):
    imag, real = left_many(tab["left"], [imag], [real])
    return real[0] * tab.turn("half", 0) - imag[0] * tab.turn("half", 1)


def load(ref, index, count):
    return ref[pl.ds(index, 128, stride=count), :]


def store(ref, index, count, block):
    ref[pl.ds(index, 128, stride=count), :] = block


def load_set(ref, base, count):
    real = [load(ref, base + k, count) for k in range(4)]
    imag = [load(ref, base + 4 + k, count) for k in range(4)]
    return real, imag


def store_set(ref, base, count, real, imag):
    for k in range(4):
        store(ref, base + k, count, real[k])
        store(ref, base + 4 + k, count, imag[k])


def block(ref, index):
    return ref[128 * index : 128 * index + 128, :]


def put(ref, index, value):
    ref[128 * index : 128 * index + 128, :] = value


class Waves:
    def __init__(self, rank, group, quarter):
        lane = lane_ids()
        column = row_ids() + 128 * (8 * (lane >> 5) + (lane & 7))
        slot = 4 * quarter + ((lane >> 3) & 3)
        if group == 1:
            slot = jnp.where(slot == 0, 16, 32 - slot)
        row = 32 * rank + slot
        self.mx = jnp.where(column < GRID // 2, column, column - GRID)
        self.my = jnp.where(row < GRID // 2, row, row - GRID)
        self.squares = self.mx * self.mx + self.my * self.my
        self.lap = self.squares.astype(jnp.float32) * (unit * unit)
        self.dx = jnp.where(column == GRID // 2, 0, self.mx).astype(jnp.float32) * unit
        self.dy = jnp.where(row == GRID // 2, 0, self.my).astype(jnp.float32) * unit

    def inverse_lap(self):
        return jnp.where(
            self.squares == 0, 0.0, 1.0 / jnp.maximum(self.lap, unit * unit)
        )

    def keep(self, cutoff):
        return (jnp.abs(self.mx) <= cutoff) & (jnp.abs(self.my) <= cutoff)

    def shell(self, radii):
        mask = None
        for radius in radii:
            inside = (radius * radius <= self.squares) & (
                self.squares < (radius + 1) * (radius + 1)
            )
            mask = inside if mask is None else mask | inside
        return mask

    def low(self):
        half = LOW // 2
        return (self.mx >= -half) & (self.mx < half) & (self.my >= -half) & (self.my < half)


def send_fields(tab, rank, state, out_ref, count, names, extra=None):
    total = len(names)
    last_real, last_imag = None, None
    lane_slot = (lane_ids() >> 3) & 3
    waves = [Waves(rank, 0, q) for q in range(4)] + [Waves(rank, 1, 0)]
    for place, name in enumerate(names):
        reals, imags = [], []
        for index in range(5):
            wave = waves[index]
            real, imag = state(0, index) if index < 4 else state(1, 0)
            if name in ("u", "v"):
                scale = wave.inverse_lap()
                real, imag = real * scale, imag * scale
            factor = {"u": wave.dy, "v": -wave.dx, "wx": wave.dx, "wy": wave.dy}[name]
            reals.append(-imag * factor)
            imags.append(real * factor)
        mine = lane_slot == place
        moved = roll(reals[4], 8 * place), roll(imags[4], 8 * place)
        last_real = jnp.where(mine, moved[0], 0.0 if last_real is None else last_real)
        last_imag = jnp.where(mine, moved[1], 0.0 if last_imag is None else last_imag)
        real, imag = x_inverse(tab, reals[:4], imags[:4])
        store_set(out_ref, 8 * place, count, swap4(real), swap4(imag))
    real, imag = x_inverse(tab, [last_real], [last_imag])
    real, imag = real[0], imag[0]
    if extra is not None:
        real, imag = extra(real, 0), extra(imag, 1)
    store(out_ref, 8 * total, count, real)
    store(out_ref, 8 * total + 1, count, imag)


FIRST = ("left", "forward_y", "turn_y", "low_rows", "turn_low")
WAVES = ("left", "right_x", "turn_x")
MIDDLE = ("left", "right_x", "turn_x", "half")
ROWS = ("left", "forward_y", "inverse_y", "turn_y", "half")
LAST = ROWS + ("coarse_y", "coarse_x")


def grid_groups(ref):
    groups = []
    for xh in range(4):
        pair = []
        for jh in range(2):
            pieces = [
                ref[8 * xh : 8 * xh + 8, 128 * j : 128 * j + 128]
                for j in range(16 * jh, 16 * jh + 16)
            ]
            pair.append(jnp.concatenate(pieces, axis=0).T)
        groups.append(pair)
    return groups


def first_kernel(vorticity_ref, forcing_ref, *rest):
    tab = Tables(FIRST, rest)
    out_ref = rest[len(FIRST)]
    direct, mirror = y_forward(tab, grid_groups(vorticity_ref))
    store_set(out_ref, 0, 17, *direct)
    store_set(out_ref, 8, 17, *mirror)
    groups = grid_groups(forcing_ref)
    values = jnp.concatenate([g[k] for g in groups for k in range(2)], axis=1)
    high, low = halves(values)
    out = dot(thrice(tab["low_rows"], 1), jnp.concatenate([high, low, high], axis=0))
    lane, row = lane_ids(), row_ids()
    sign = jnp.where((row & 1) == 0, 1.0, -1.0)
    cos, sin = tab.turn("turn_low", 0), tab.turn("turn_low", 1)
    packed = jnp.zeros((128, 128), jnp.float32)
    for xh in range(4):
        at = 256 * xh
        real = out[:128, at : at + 128] + sign * out[:128, at + 128 : at + 256]
        imag = out[128:, at : at + 128] + sign * out[128:, at + 128 : at + 256]
        for part, value in enumerate(turned(real, imag, cos, sin)):
            for shift in (64, 32, 16, 8):
                value = value + roll(value, shift)
            mine = ((lane >> 5) == xh) & (((lane >> 3) & 3) == part)
            packed = jnp.where(mine, value, packed)
    store(out_ref, 16, 17, packed)


def start_kernel(scalars, in_ref, *rest):
    tab = Tables(WAVES, rest)
    state_ref, out_ref = rest[len(WAVES) :]
    rank = scalars[0]
    for group in range(2):
        real, imag = x_forward(tab, *load_set(in_ref, 8 * group, 17))
        for q in range(4):
            put(state_ref, 8 * group + 2 * q, real[q])
            put(state_ref, 8 * group + 2 * q + 1, imag[q])
    row = load(in_ref, 16, 17)
    lane = lane_ids()
    part = (lane >> 3) & 3
    real = jnp.where(part == 0, row, jnp.where(part == 1, roll(row, 8), 0.0))
    imag = jnp.where(part == 0, roll(row, -8), jnp.where(part == 1, -row, 0.0))
    real, imag = x_plain(tab, [real], [imag])

    def extra(values, which):
        source = (real, imag)[which][0]
        for spot, origin in enumerate((0, 103, 8, 111)):
            moved = roll(source, 24 + spot - origin)
            values = jnp.where(lane == 24 + spot, moved, values)
        return values

    state = lambda group, q: (
        block(state_ref, 8 * group + 2 * q),
        block(state_ref, 8 * group + 2 * q + 1),
    )
    send_fields(tab, rank, state, out_ref, 26, ("u", "v", "wx"), extra)


def product_one(tab, in_ref, count, last, place):
    real, imag = load_set(in_ref, 8 * place, count)
    return y_inverse(tab, real, imag, last, place)


def drive_rows(real, imag):
    lane = lane_ids()
    columns = jnp.where(lane < 4, roll(real, -24), roll(imag, -20)).T
    pick = lambda index: jnp.broadcast_to(columns[index : index + 1, :], (8, 128))
    plus = swap4([pick(4 * part + k) for part in range(2) for k in range(2)])
    minus = swap4([pick(4 * part + 2 + k) for part in range(2) for k in range(2)])
    sub = lax.broadcasted_iota(jnp.int32, (8, 128), 0)
    start = (lax.broadcasted_iota(jnp.int32, (8, 128), 1) & 31) == 0
    top = jnp.zeros((8, 128), jnp.float32)
    bottom = jnp.zeros((8, 128), jnp.float32)
    for k in range(4):
        top = jnp.where(sub == k, plus[k], top)
        after = minus[k + 1] if k < 3 else 0.0
        bottom = jnp.where(sub == 7 - k, jnp.where(start, after, minus[k]), bottom)
    return jnp.concatenate([top, jnp.zeros((112, 128), jnp.float32), bottom], axis=0)


def product_first_kernel(in_ref, local_ref, *rest):
    tab = Tables(ROWS, rest)
    out_ref = rest[len(ROWS)]
    last_real, last_imag = load(in_ref, 24, 26), load(in_ref, 25, 26)
    store(out_ref, 16, 17, drive_rows(last_real, last_imag))
    last = last_row(tab, last_real, last_imag)
    u0, u1 = product_one(tab, in_ref, 26, last, 0)
    x0, x1 = product_one(tab, in_ref, 26, last, 2)
    sum0 = [a * b for a, b in zip(u0, x0)]
    sum1 = [a * b for a, b in zip(u1, x1)]
    lane = lane_ids()
    row = 32 * row_ids() + (lane >> 3)
    slope = jnp.where(row < GRID // 2, row, row - GRID)
    slope = jnp.where(row == GRID // 2, 0, slope).astype(jnp.float32) * unit
    real, imag = load_set(local_ref, 0, 17)
    real, imag = [-b * slope for b in imag], [a * slope for a in real]
    row = 32 * row_ids() + 16
    slope = jnp.where(row < GRID // 2, row, row - GRID).astype(jnp.float32) * unit
    last_real, last_imag = 0.0, 0.0
    for xh in range(4):
        mine = (lane >> 3) == 4 * xh
        a, b = load(local_ref, 8 + xh, 17), load(local_ref, 12 + xh, 17)
        last_real = jnp.where(mine, roll(-b * slope, 32 * xh), last_real)
        last_imag = jnp.where(mine, roll(a * slope, 32 * xh), last_imag)
    own = last_row(tab, last_real, last_imag)
    y0, y1 = y_inverse(tab, real, imag, own, 0)
    v0, v1 = product_one(tab, in_ref, 26, last, 1)
    sum0 = [s + a * b for s, a, b in zip(sum0, v0, y0)]
    sum1 = [s + a * b for s, a, b in zip(sum1, v1, y1)]
    direct, mirror = y_forward(tab, list(zip(sum0, sum1)))
    store_set(out_ref, 0, 17, *direct)
    store_set(out_ref, 8, 17, *mirror)


def product_kernel(scalars, in_ref, *rest):
    tab = Tables(LAST, rest)
    out_ref, mixed_ref = rest[len(LAST) :]
    got = load(in_ref, 34, 35)
    mixed_ref[0:4, :] = got[0:4, :]
    mixed_ref[4:8, :] = got[124:128, :]
    last = last_row(tab, load(in_ref, 32, 35), load(in_ref, 33, 35))
    sum0, sum1 = None, None
    for one, two in ((0, 2), (1, 3)):
        a0, a1 = product_one(tab, in_ref, 35, last, one)
        b0, b1 = product_one(tab, in_ref, 35, last, two)
        made0 = [a * b for a, b in zip(a0, b0)]
        made1 = [a * b for a, b in zip(a1, b1)]
        sum0 = made0 if sum0 is None else [s + m for s, m in zip(sum0, made0)]
        sum1 = made1 if sum1 is None else [s + m for s, m in zip(sum1, made1)]
    direct, mirror = y_forward(tab, list(zip(sum0, sum1)))
    store_set(out_ref, 0, 20, *direct)
    store_set(out_ref, 8, 20, *mirror)
    pieces = []
    for xh in range(4):
        for part in (direct[0], direct[1], mirror[0], mirror[1]):
            pieces.append(part[xh][0:8, :])
    across = jnp.concatenate(pieces, axis=0).T
    made = [
        swap4([across[8 * t : 8 * t + 8, :] for t in range(4 * tq, 4 * tq + 4)])
        for tq in range(4)
    ]
    values = jnp.concatenate(
        [jnp.concatenate([made[tq][xh] for tq in range(4)], axis=1) for xh in range(4)],
        axis=0,
    )
    high, low = halves(values)
    points = dot(
        jnp.concatenate([high, low, high], axis=1), thrice(tab["coarse_y"], 0)
    )
    flip = lax.broadcasted_iota(jnp.int32, (32, LOW), 1) & 1
    edge = jnp.where(flip == 0, 1.0, -1.0) * values[:, 12:13]
    high, low = halves(jnp.concatenate([points, edge], axis=0))
    share = dot(
        tab["coarse_x"], jnp.concatenate([high, low, high, jnp.zeros_like(low)], axis=0)
    )
    for odd in range(2):
        for side in range(2):
            piece = share[128 * odd : 128 * odd + 128, 128 * side : 128 * side + 128]
            piece = pltpu.roll(piece, scalars[0], 0)
            store(out_ref, 16 + 2 * odd + side, 20, piece)


def drive_blocks(rank, values):
    shape = (128, 128)
    source = row_ids()
    lane = lane_ids()
    number = 8 * (lane >> 5) + (lane & 7)
    side = jnp.where(number == 0, 0, jnp.where(number == 31, 1, 4))
    made = []
    for group in range(2):
        for q in range(4):
            slot = 4 * q + ((lane >> 3) & 3)
            back = jnp.where(slot == 0, 16 * group, 32 - slot)
            near, far = (slot, back) if group == 0 else (back, jnp.where(slot == 0, 16, slot))
            slot = jnp.where(rank < 64, near, far)
            for part in range(2):
                want = 64 * part + 32 * side + slot
                want = jnp.where(side == 4, -1, want)
                made.append(jnp.where(source == want, 1.0, 0.0).astype(jnp.bfloat16))
    select = jnp.concatenate(made, axis=1)
    high, low = halves(values)
    out = dot(
        jnp.concatenate([high, low], axis=1), jnp.concatenate([select, select], axis=0)
    )
    return lambda place: out[:, 128 * place : 128 * place + 128]


def middle_kernel(scalars, in_ref, state_ref, *rest):
    tab = Tables(MIDDLE, rest)
    ahead_ref, out_ref, next_ref = rest[len(MIDDLE) :]
    rank, cutoff = scalars[0], scalars[1]
    radii = [scalars[2 + k] for k in range(SHELLS)]
    lane = lane_ids()
    drive_of = drive_blocks(rank, load(in_ref, 16, 17))
    low0 = [0.0, 0.0]
    low1 = [0.0, 0.0]
    for group in range(2):
        real, imag = x_forward(tab, *load_set(in_ref, 8 * group, 17))
        for q in range(4):
            wave = Waves(rank, group, q)
            keep = wave.keep(cutoff)
            shell = wave.shell(radii)
            low = wave.low()
            damp = viscosity * wave.lap
            spot = 4 * group + q
            mine = (lane < 32) & ((lane & 7) == spot)
            for part, term in enumerate((real[q], imag[q])):
                place = 8 * group + 2 * q + part
                now = block(state_ref, place)
                drive = jnp.where(shell, drive_of(place), 0.0)
                slope = drive - jnp.where(keep, term, 0.0) - damp * now
                after = now + time_step * slope
                put(next_ref, place, after)
                rest_slope = slope + drive - damp * after
                done = now + 0.5 * time_step * rest_slope
                lifted = jnp.where(low, done + coarse_ratio * (done - now), done)
                put(ahead_ref, place, lifted)
                lifted = jnp.where(low, lifted, 0.0)
                low0[part] = jnp.where(mine, roll(lifted, spot), low0[part])
                low1[part] = jnp.where(mine, roll(lifted, 25 + spot), low1[part])
    even = [a + b for a, b in zip(low0, low1)]
    odd = [a - b for a, b in zip(low0, low1)]
    cos, sin = tab.turn("half", 0), tab.turn("half", 1)
    odd = [odd[0] * cos - odd[1] * sin, odd[0] * sin + odd[1] * cos]
    both = [jnp.where(lane < 32, e, roll(o, 32)) for e, o in zip(even, odd)]
    both = [jnp.where(lane < 64, b, 0.0) for b in both]
    second, first = left_many(tab["left"], [both[1]], [both[0]])
    store(out_ref, 34, 35, jnp.where(lane < 64, first[0], roll(second[0], 64)))
    state = lambda group, q: (
        block(next_ref, 8 * group + 2 * q),
        block(next_ref, 8 * group + 2 * q + 1),
    )
    send_fields(tab, rank, state, out_ref, 35, ("u", "v", "wx", "wy"))


def final_kernel(scalars, in_ref, ahead_ref, coarse_ref, *rest):
    tab = Tables(WAVES, rest)
    out_ref, points_ref = rest[len(WAVES) :]
    rank, cutoff = scalars[0], scalars[1]
    for odd in range(2):
        for side in range(2):
            total = jnp.sum(load(in_ref, 16 + 2 * odd + side, 20), axis=0, keepdims=True)
            at = slice(128 * side, 128 * side + 128)
            points_ref[odd : odd + 1, at] = coarse_ref[odd : odd + 1, at] + total
    for group in range(2):
        real, imag = x_forward(tab, *load_set(in_ref, 8 * group, 20))
        for q in range(4):
            wave = Waves(rank, group, q)
            factor = jnp.where(wave.low(), (1 + coarse_ratio) * 0.5 * time_step, 0.5 * time_step)
            factor = jnp.where(wave.keep(cutoff), factor, 0.0)
            for part, term in enumerate((real[q], imag[q])):
                lifted = block(ahead_ref, 8 * group + 2 * q + part) - factor * term
                flipped = lifted.T
                for kh in range(4):
                    for slot in range(4):
                        at = 32 * kh + 8 * slot
                        piece = flipped[at : at + 8, :]
                        number = 4 * q + slot
                        if group == 1:
                            number = 16 if number == 0 else 32 - number
                        for kl in range(8):
                            col = 128 * (8 * kh + kl)
                            out_ref[part, number, col : col + 128] = piece[kl]


VMEM = pl.BlockSpec(memory_space=pltpu.VMEM)
SMEM = pl.BlockSpec(memory_space=pltpu.SMEM)


def call(kernel, name, outs, args, scalar=False):
    specs = [SMEM] if scalar else []
    specs = specs + [VMEM] * (len(args) - len(specs))
    return pl.pallas_call(
        kernel,
        name=name,
        out_shape=[jax.ShapeDtypeStruct(shape, jnp.float32) for shape in outs],
        in_specs=specs,
        out_specs=[VMEM] * len(outs),
        compiler_params=pltpu.CompilerParams(vmem_limit_bytes=VMEM_LIMIT * 1024 * 1024),
    )(*args)


def exchange(buffer, count):
    cut = buffer.reshape(128, 1, count * 128)
    cut = lax.all_to_all(cut, AXES, split_axis=0, concat_axis=0, tiled=True)
    return cut.reshape(128 * count, 128)


@functools.lru_cache(None)
def coarse_table():
    source = np.array([0, 1, 2, 3, 124, 125, 126, 127])
    slot = np.arange(32)
    inner, spot = slot >> 3, slot & 7
    number = 4 * (spot & 3) + inner
    row = np.where(spot < 4, number, np.where(number == 0, 16, 32 - number))
    wave = 32 * source[:, None] + row[None, :]
    angle = 2 * np.pi * ((wave[:, :, None] * np.arange(LOW)) % LOW) / LOW
    return (np.stack([np.cos(angle), -np.sin(angle)], axis=1) * (8 / LOW)).astype(np.float32)


def body(vorticity_grid, forcing_grid, cutoff, forcing_shells):
    rank = lax.axis_index("gx") * lax.axis_size("gy") + lax.axis_index("gy")
    scalars = jnp.concatenate([rank[None].astype(jnp.int32), cutoff, forcing_shells])
    made = {name: jnp.asarray(table) for name, table in tables().items()}
    tabs = lambda names: tuple(made[name] for name in names)
    spectrum = (16 * 128, 128)
    (sent,) = call(
        first_kernel, "first", [(128 * 17, 128)], (vorticity_grid, forcing_grid) + tabs(FIRST)
    )
    got = exchange(sent, 17)
    state, fields = call(
        start_kernel, "start", [spectrum, (128 * 26, 128)], (scalars, got) + tabs(WAVES), True
    )
    got = exchange(fields, 26)
    (term,) = call(
        product_first_kernel, "product_first", [(128 * 17, 128)], (got, sent) + tabs(ROWS)
    )
    got = exchange(term, 17)
    ahead, fields, _ = call(
        middle_kernel,
        "middle",
        [spectrum, (128 * 35, 128), spectrum],
        (scalars, got, state) + tabs(MIDDLE),
        True,
    )
    got = exchange(fields, 35)
    term, mixed = call(
        product_kernel,
        "product",
        [(128 * 20, 128), (8, 128)],
        (scalars, got) + tabs(LAST),
        True,
    )
    got = exchange(term, 20)
    coarse = jnp.einsum(
        "sceq,scqb->eb",
        mixed.reshape(8, 2, 2, 32),
        jnp.asarray(coarse_table()),
        precision=lax.Precision.HIGHEST,
    )
    lifted, coarse = call(
        final_kernel,
        "final",
        [(2, 32, GRID), (2, LOW)],
        (scalars, got, ahead, coarse) + tabs(WAVES),
        True,
    )
    return lifted, coarse


def solution(mesh):
    placed = (P(AXES, None), P(AXES, None), P(), P())
    return jax.shard_map(
        body,
        mesh=mesh,
        in_specs=placed,
        out_specs=(P(None, AXES, None), P(AXES, None)),
        check_vma=False,
    )
```

time: 663 us -> 183 us (0.28); the launches traced: 652 us -> 182 us
  local copies, waits for them, and re-layouts: 258 us -> 7.48 us
  matrix products: 107 us -> 1.05 us
  waiting for transfers between devices: 111 us -> 40.6 us
  other arithmetic: 58.8 us -> 0.08 us
  Pallas kernels: 0 us -> 26.9 us
  between operations: 23.3 us -> 1.42 us
  blocking collectives: 71.8 us -> 89.7 us
    dot_general x26 -> x1, matrix products: 107 us -> 1.05 us  [body(): jnp.einsum('sceq,scqb->eb', mixed.reshape(8, 2, 2, 32), jnp.asarray(coars...]
    another operation x12 -> x0, local copies, waits for them, and re-layouts: 77.5 us -> none  [the longest x3 25.7 us: forward(): moved = rows_to_waves(half.reshape((2 * field_count,) + half.shape[2:]))]
    unnamed x48 -> x36, local copies, waits for them, and re-layouts: 73.1 us -> 6.79 us
    all_gather x1 -> x0, waiting for transfers between devices: 63.9 us -> none  [body(): every_row = lax.all_gather(low_columns, ('gx', 'gy'), axis=1, tiled=True)]
    all_to_all x9 -> x0, local copies, waits for them, and re-layouts: 62.7 us -> none  [the longest x7 39.8 us: rows_to_waves(): lax.all_to_all(packed, ('gx', 'gy'), split_axis=2, concat_axis=1, tiled=T...]
    all_to_all x5 -> x0, other arithmetic: 34.4 us -> none  [the longest x2 17.4 us: rows_to_grid(): lax.all_to_all(packed, ('gx', 'gy'), split_axis=1, concat_axis=2, tiled=T...]
    pallas_call x0 -> x6, Pallas kernels: none -> 26.9 us  [call(): pl.pallas_call(kernel, name=name, out_shape=[jax.ShapeDtypeStruct(shape,...]
    all_to_all x2 -> x3, blocking collectives: 71.8 us -> 89.7 us  [exchange(): cut = lax.all_to_all(cut, AXES, split_axis=0, concat_axis=0, tiled=True)]
  transfers between devices with their start and end apart: 4 -> 2, of which waited for: 4 -> 2; matrix products, arithmetic and copies ran while one was open for 2% -> 1% of each run, Pallas kernels for 0% -> 0%
where the time goes in v1:
time: 183 us; the launch traced here: 182 us
  blocking collectives  89.7 us (49%)
  waiting for transfers between devices  40.6 us (22%)
  Pallas kernels  26.9 us (15%)
  starting transfers between devices  15.2 us (8%)
  local copies, waits for them, and re-layouts  7.48 us (4%)
    all_to_all x3, blocking collectives, exchange(): cut = lax.all_to_all(cut, AXES, split_axis=0, concat_axis=0, tiled=True)  89.7 us
    all_to_all x2, waiting for transfers between devices, exchange(): cut = lax.all_to_all(cut, AXES, split_axis=0, concat_axis=0, tiled=True)  40.6 us
    pallas_call x6, Pallas kernels, call(): pl.pallas_call(kernel, name=name, out_shape=[jax.ShapeDtypeStruct(shape,...  26.9 us
    all_to_all x2, starting transfers between devices, exchange(): cut = lax.all_to_all(cut, AXES, split_axis=0, concat_axis=0, tiled=True)  15.2 us
    unnamed x36, local copies, waits for them, and re-layouts  6.79 us
  transfers between devices with their start and end apart: 2, of which 2 were waited for; matrix products, arithmetic and copies ran while one was open for 1% of the time, Pallas kernels for 0%

profile of v1, /device:TPU:1, one launch (start us, length us, event | category | flops | bytes accessed | tf_op | source)
XLA Modules:
  0.0 182.5 jit_solution(14169774334384201923)
XLA Ops:
  0.6 0.0 copy-start
  0.6 0.9 copy-done
  1.6 0.9 copy-done.2
  2.5 0.9 copy-done.4
  3.5 1.0 copy-done.10
  4.5 1.0 copy-done.11
  5.6 0.9 copy-done.14
  6.5 0.9 copy-done.15
  7.4 2.9 %first.1.local_ref = f32[2176,128]{1,0:T(8,128)} custom-call(f32[32,4096]{1,0:T(8,128)S(1)} %copy-done.10, f32[32,4096]{1,0:T(8,128)S(1)} %copy-done.11, bf16[256,512]{1,0:T(8,128)(2,1)S(1)} %copy-done, bf16[512,256]{1,0:T(8,128)(2,1)S(1)} %copy-done.4, f32[512,128]{1,0:T(8,128)S(1)} %copy-done.2, bf16[256,256]{1,0:T(8,128)(2,1)S(1)} %copy-done.15, ...), custom_call_target="tpu_custom_call" | custom-call | tf_op jit(solution)/shard_map/first/pallas_call | solution.py:637
  10.3 11.5 %all-to-all-start = ((f32[128,1,2176]{2,1,0:T(1,128)}), f32[128,1,2176]{2,1,0:T(1,128)S(1)}, u32[]{:S(2)}, u32[]{:S(2)}) async-start(f32[128,1,2176]{2,1,0:T(1,128)} %bitcast.1), calls=%async_computation | async-start | bytes 2228224 | tf_op jit(solution)/shard_map/all_to_all | solution.py:649
  22.5 0.1 pad_add_fusion.scalars
  22.6 19.7 %all-to-all-done = f32[128,1,2176]{2,1,0:T(1,128)S(1)} async-done(((f32[128,1,2176]{2,1,0:T(1,128)}), f32[128,1,2176]{2,1,0:T(1,128)S(1)}, u32[]{:S(2)}, u32[]{:S(2)}) %all-to-all-start) | async-done | bytes 1114144 | tf_op jit(solution)/shard_map/all_to_all | solution.py:649
  42.3 0.0 copy-done.8
  42.3 4.0 %start.1 = (f32[2048,128]{1,0:T(8,128)S(1)}, f32[3328,128]{1,0:T(8,128)S(1)}) custom-call(s32[6]{0:T(128)S(1)} %pad_add_fusion.scalars, f32[2176,128]{1,0:T(8,128)S(1)} %bitcast.20, bf16[256,512]{1,0:T(8,128)(2,1)S(1)} %copy-done.1, bf16[512,256]{1,0:T(8,128)(2,1)S(1)} %copy-done.6, f32[256,128]{1,0:T(8,128)S(1)} %copy-done.8), custom_call_target="tpu_custom_call" | custom-call | tf_op jit(solution)/shard_map/start/pallas_call | solution.py:637
  46.3 0.0 copy-start.3
  46.3 0.0 copy-start.5
  46.3 0.0 copy-start.7
  46.3 0.0 copy-start.9
  46.3 30.0 %all_to_all.25 = f32[128,1,3328]{2,1,0:T(1,128)S(1)} all-to-all(f32[128,1,3328]{2,1,0:T(1,128)S(1)} %bitcast.23), channel_id=1, replica_groups=mesh['gx'=32,'gy'=4] {'gx','gy'}, dimensions={0} | all-to-all | bytes 3407872 | tf_op jit(solution)/shard_map/all_to_all | solution.py:649
  76.3 0.0 copy-done.5
  76.3 4.8 %product_first.1 = f32[2176,128]{1,0:T(8,128)S(1)} custom-call(f32[3328,128]{1,0:T(8,128)S(1)} %bitcast.17, f32[2176,128]{1,0:T(8,128)} %first.1.local_ref, bf16[256,512]{1,0:T(8,128)(2,1)S(1)} %copy-done.1, bf16[512,256]{1,0:T(8,128)(2,1)S(1)} %copy-done.5, bf16[512,256]{1,0:T(8,128)(2,1)S(1)} %copy-done.9, f32[512,128]{1,0:T(8,128)S(1)} %copy-done.3, ...), custom_call_target="tpu_custom_call" | custom-call | tf_op jit(solution)/shard_map/product_first/pallas_call | solution.py:637
  81.2 23.5 %all_to_all.26 = f32[128,1,2176]{2,1,0:T(1,128)S(1)} all-to-all(f32[128,1,2176]{2,1,0:T(1,128)S(1)} %bitcast.19), channel_id=1, replica_groups=mesh['gx'=32,'gy'=4] {'gx','gy'}, dimensions={0} | all-to-all | bytes 2228224 | tf_op jit(solution)/shard_map/all_to_all | solution.py:649
  104.7 5.9 %middle.1 = (f32[2048,128]{1,0:T(8,128)S(1)}, f32[4480,128]{1,0:T(8,128)S(1)}, f32[2048,128]{1,0:T(8,128)}) custom-call(s32[6]{0:T(128)S(1)} %pad_add_fusion.scalars, f32[2176,128]{1,0:T(8,128)S(1)} %bitcast.21, f32[2048,128]{1,0:T(8,128)S(1)} %get-tuple-element.9.state_ref, bf16[256,512]{1,0:T(8,128)(2,1)S(1)} %copy-done.1, bf16[512,256]{1,0:T(8,128)(2,1)S(1)} %copy-done.6, ...), custom_call_target="tpu_custom_call" | custom-call | tf_op jit(solution)/shard_map/middle/pallas_call | solution.py:637
  110.6 0.0 copy-start.12
  110.6 0.0 copy-start.13
  110.6 36.3 %all_to_all.27 = f32[128,1,4480]{2,1,0:T(1,128)S(1)} all-to-all(f32[128,1,4480]{2,1,0:T(1,128)S(1)} %bitcast.22), channel_id=1, replica_groups=mesh['gx'=32,'gy'=4] {'gx','gy'}, dimensions={0} | all-to-all | bytes 4587520 | tf_op jit(solution)/shard_map/all_to_all | solution.py:649
  146.9 5.6 %product.1 = (f32[2560,128]{1,0:T(8,128)}, f32[8,128]{1,0:T(8,128)S(1)}) custom-call(s32[6]{0:T(128)S(1)} %pad_add_fusion.scalars, f32[4480,128]{1,0:T(8,128)S(1)} %bitcast.16, bf16[256,512]{1,0:T(8,128)(2,1)S(1)} %copy-done.1, bf16[512,256]{1,0:T(8,128)(2,1)S(1)} %copy-done.5, bf16[512,256]{1,0:T(8,128)(2,1)S(1)} %copy-done.9, f32[512,128]{1,0:T(8,128)S(1)} %copy-done.3, ...), custom_call_target="tpu_custom_call" | custom-call | tf_op jit(solution)/shard_map/product/pallas_call | solution.py:637
  152.5 3.7 %all-to-all-start.4 = ((f32[128,1,2560]{2,1,0:T(1,128)}), f32[128,1,2560]{2,1,0:T(1,128)S(1)}, u32[]{:S(2)}, u32[]{:S(2)}) async-start(f32[128,1,2560]{2,1,0:T(1,128)} %bitcast.9), calls=%async_computation.4 | async-start | bytes 2621440 | tf_op jit(solution)/shard_map/all_to_all | solution.py:649
  156.2 0.7 reshape.47
  156.9 1.0 convolution_bitcast_fusion.coarse_ref
  158.0 20.9 %all-to-all-done.4 = f32[128,1,2560]{2,1,0:T(1,128)S(1)} async-done(((f32[128,1,2560]{2,1,0:T(1,128)}), f32[128,1,2560]{2,1,0:T(1,128)S(1)}, u32[]{:S(2)}, u32[]{:S(2)}) %all-to-all-start.4) | async-done | bytes 1310752 | tf_op jit(solution)/shard_map/all_to_all | solution.py:649
  178.9 3.6 %final.1 = (f32[2,32,4096]{2,1,0:T(8,128)}, f32[2,256]{1,0:T(2,128)}) custom-call(s32[6]{0:T(128)S(1)} %pad_add_fusion.scalars, f32[2560,128]{1,0:T(8,128)S(1)} %bitcast.18, f32[2048,128]{1,0:T(8,128)S(1)} %get-tuple-element.12.ahead_ref, f32[2,256]{1,0:T(2,128)S(1)} %convolution_bitcast_fusion.coarse_ref, bf16[256,512]{1,0:T(8,128)(2,1)S(1)} %copy-done.1, ...), custom_call_target="tpu_custom_call" | custom-call | tf_op jit(solution)/shard_map/final/pallas_call | solution.py:637
  (20 shorter events, 0.0 us)
Async XLA Ops:
  0.6 1.0 copy-start
  1.6 0.9 copy-start.2
  2.5 0.9 copy-start.4
  3.5 1.0 copy-start.10
  4.5 1.0 copy-start.11
  5.6 0.9 copy-start.14
  6.5 0.9 copy-start.15
  10.3 12.2 %copy-start.17 = (s32[4]{0:T(128)S(1)}, s32[4]{0:T(128)}, u32[]{:S(2)}) copy-start(s32[4]{0:T(128)} %param.19) | copy-start | bytes 52
  10.3 31.9 %copy-start.1 = (bf16[256,512]{1,0:T(8,128)(2,1)S(1)}, bf16[256,512]{1,0:T(8,128)(2,1)}, u32[]{:S(2)}) copy-start(bf16[256,512]{1,0:T(8,128)(2,1)} %constant.35.clone.rest_0_) | copy-start | bytes 786436
  10.3 31.9 %copy-start.6 = (bf16[512,256]{1,0:T(8,128)(2,1)S(1)}, bf16[512,256]{1,0:T(8,128)(2,1)}, u32[]{:S(2)}) copy-start(bf16[512,256]{1,0:T(8,128)(2,1)} %constant.36.clone.rest_1_) | copy-start | bytes 786436
  10.3 31.9 %copy-start.8 = (f32[256,128]{1,0:T(8,128)S(1)}, f32[256,128]{1,0:T(8,128)}, u32[]{:S(2)}) copy-start(f32[256,128]{1,0:T(8,128)} %constant.39.clone.rest_2_) | copy-start | bytes 393220
  10.3 31.9 %all-to-all-start = ((f32[128,1,2176]{2,1,0:T(1,128)}), f32[128,1,2176]{2,1,0:T(1,128)S(1)}, u32[]{:S(2)}, u32[]{:S(2)}) async-start(f32[128,1,2176]{2,1,0:T(1,128)} %bitcast.1), calls=%async_computation | async-start | bytes 2228224 | tf_op jit(solution)/shard_map/all_to_all | solution.py:649
  46.3 30.0 %copy-start.3 = (f32[512,128]{1,0:T(8,128)S(1)}, f32[512,128]{1,0:T(8,128)}, u32[]{:S(2)}) copy-start(f32[512,128]{1,0:T(8,128)} %constant.40.clone.rest_2_.rest_3_) | copy-start | bytes 786436
  46.3 30.0 %copy-start.5 = (bf16[512,256]{1,0:T(8,128)(2,1)S(1)}, bf16[512,256]{1,0:T(8,128)(2,1)}, u32[]{:S(2)}) copy-start(bf16[512,256]{1,0:T(8,128)(2,1)} %constant.37.clone.rest_1_) | copy-start | bytes 786436
  46.3 30.0 %copy-start.7 = (f32[256,128]{1,0:T(8,128)S(1)}, f32[256,128]{1,0:T(8,128)}, u32[]{:S(2)}) copy-start(f32[256,128]{1,0:T(8,128)} %constant.41.clone.rest_4_.rest_3_) | copy-start | bytes 393220
  46.3 30.0 %copy-start.9 = (bf16[512,256]{1,0:T(8,128)(2,1)S(1)}, bf16[512,256]{1,0:T(8,128)(2,1)}, u32[]{:S(2)}) copy-start(bf16[512,256]{1,0:T(8,128)(2,1)} %constant.38.clone.rest_2_) | copy-start | bytes 786436
  110.6 36.3 %copy-start.12 = (bf16[1024,256]{1,0:T(8,128)(2,1)S(1)}, bf16[1024,256]{1,0:T(8,128)(2,1)}, u32[]{:S(2)}) copy-start(bf16[1024,256]{1,0:T(8,128)(2,1)} %constant.44.clone.rest_5_) | copy-start | bytes 1572868
  110.6 36.3 %copy-start.13 = (bf16[256,256]{1,0:T(8,128)(2,1)S(1)}, bf16[256,256]{1,0:T(8,128)(2,1)}, u32[]{:S(2)}) copy-start(bf16[256,256]{1,0:T(8,128)(2,1)} %constant.45.clone.rest_6_) | copy-start | bytes 393220
  152.5 4.4 %copy-start.16 = (f32[8,2,32,256]{3,2,0,1:T(8,128)S(1)}, f32[8,2,32,256]{3,2,0,1:T(8,128)}, u32[]{:S(2)}) copy-start(f32[8,2,32,256]{3,2,0,1:T(8,128)} %constant.46.clone) | copy-start | bytes 1572868
  152.5 26.4 %all-to-all-start.4 = ((f32[128,1,2560]{2,1,0:T(1,128)}), f32[128,1,2560]{2,1,0:T(1,128)S(1)}, u32[]{:S(2)}, u32[]{:S(2)}) async-start(f32[128,1,2560]{2,1,0:T(1,128)} %bitcast.9), calls=%async_computation.4 | async-start | bytes 2621440 | tf_op jit(solution)/shard_map/all_to_all | solution.py:649

commit v2 on v1

--- a/solution.py
+++ b/solution.py
@@ -65,6 +65,46 @@
     made["turn_y"] = planes([np.cos(turn_d), np.sin(turn_d), np.cos(turn_m), np.sin(turn_m)])
     half = 2 * np.pi * rows / 256 + np.zeros((128, 128))
     made["half"] = planes([np.cos(half), np.sin(half)])
+
+    column = rows + 128 * inner[None, :]
+    mx = np.where(column < GRID // 2, column, column - GRID)
+    made["wave_x"] = planes(
+        [
+            np.where(column == GRID // 2, 0, mx) * unit,
+            mx * mx,
+            np.where((mx >= -LOW // 2) & (mx < LOW // 2), 1.0, 0.0),
+        ]
+    )
+
+    spot = np.arange(32)
+    inside, group, quarter = spot >> 3, (spot >> 2) & 1, spot & 3
+    number = 4 * quarter + inside
+    number = np.where(group == 0, number, np.where(number == 0, 16, 32 - number))
+    made["drive_spots"] = np.concatenate(
+        [
+            np.kron(np.eye(4), index[:32, None] == want[None, :])
+            for want in (number, (32 - number) % 32)
+        ],
+        axis=0,
+    ).astype(jnp.bfloat16)
+
+    point = np.arange(LOW)[None, :]
+    angle = 2 * np.pi * (np.tile(number, 4)[:, None] * point % LOW) / LOW
+    plain = ((lane >> 5) & 1 == 0)[:, None] * (8 / LOW)
+    imag = (lane >= 64)[:, None]
+    made["coarse_rows"] = split_np(
+        np.concatenate(
+            [
+                plain * np.where(imag, -np.sin(angle), np.cos(angle)),
+                plain * np.where(imag, np.cos(angle), np.sin(angle)),
+            ],
+            axis=1,
+        ),
+        0,
+    )
+    source = np.array([0, 1, 2, 3, 124, 125, 126, 127])[:, None]
+    angle = 2 * np.pi * (source * point % 8) / 8
+    made["coarse_turn"] = planes([np.cos(angle), -np.sin(angle)])
 
     angle = 2 * np.pi * np.outer(index, index) / GRID
     low = np.concatenate([np.cos(angle), -np.sin(angle)], axis=0) / 64
@@ -276,59 +316,58 @@
     ref[128 * index : 128 * index + 128, :] = value
 
 
-class Waves:
+def rank_here():
+    return lax.axis_index("gx") * lax.axis_size("gy") + lax.axis_index("gy")
+
+
+class Rows:
     def __init__(self, rank, group, quarter):
-        lane = lane_ids()
-        column = row_ids() + 128 * (8 * (lane >> 5) + (lane & 7))
+        lane = lax.broadcasted_iota(jnp.int32, (1, 128), 1)
         slot = 4 * quarter + ((lane >> 3) & 3)
         if group == 1:
             slot = jnp.where(slot == 0, 16, 32 - slot)
         row = 32 * rank + slot
-        self.mx = jnp.where(column < GRID // 2, column, column - GRID)
-        self.my = jnp.where(row < GRID // 2, row, row - GRID)
-        self.squares = self.mx * self.mx + self.my * self.my
-        self.lap = self.squares.astype(jnp.float32) * (unit * unit)
-        self.dx = jnp.where(column == GRID // 2, 0, self.mx).astype(jnp.float32) * unit
-        self.dy = jnp.where(row == GRID // 2, 0, self.my).astype(jnp.float32) * unit
-
-    def inverse_lap(self):
-        return jnp.where(
-            self.squares == 0, 0.0, 1.0 / jnp.maximum(self.lap, unit * unit)
-        )
+        my = jnp.where(row < GRID // 2, row, row - GRID)
+        self.my = my
+        self.square = (my * my).astype(jnp.float32)
+        self.slope = jnp.where(row == GRID // 2, 0, my).astype(jnp.float32) * unit
 
     def keep(self, cutoff):
-        return (jnp.abs(self.mx) <= cutoff) & (jnp.abs(self.my) <= cutoff)
-
-    def shell(self, radii):
-        mask = None
-        for radius in radii:
-            inside = (radius * radius <= self.squares) & (
-                self.squares < (radius + 1) * (radius + 1)
-            )
-            mask = inside if mask is None else mask | inside
-        return mask
+        return jnp.where(jnp.abs(self.my) <= cutoff, 1.0, 0.0)
 
     def low(self):
         half = LOW // 2
-        return (self.mx >= -half) & (self.mx < half) & (self.my >= -half) & (self.my < half)
+        return jnp.where((self.my >= -half) & (self.my < half), 1.0, 0.0)
+
+
+def keep_columns(tab, cutoff):
+    return jnp.where(tab.turn("wave_x", 1) <= (cutoff * cutoff).astype(jnp.float32), 1.0, 0.0)
 
 
 def send_fields(tab, rank, state, out_ref, count, names, extra=None):
     total = len(names)
     last_real, last_imag = None, None
     lane_slot = (lane_ids() >> 3) & 3
-    waves = [Waves(rank, 0, q) for q in range(4)] + [Waves(rank, 1, 0)]
+    rows = [Rows(rank, 0, q) for q in range(4)] + [Rows(rank, 1, 0)]
+    across, squares = tab.turn("wave_x", 0), tab.turn("wave_x", 1)
+    sources = {}
+    for index in range(5):
+        real, imag = state(0, index) if index < 4 else state(1, 0)
+        both = squares + rows[index].square
+        scale = jnp.where(both == 0.0, 0.0, (1.0 / (unit * unit)) / jnp.maximum(both, 1.0))
+        sources["w", index] = real, imag
+        sources["psi", index] = real * scale, imag * scale
     for place, name in enumerate(names):
         reals, imags = [], []
         for index in range(5):
-            wave = waves[index]
-            real, imag = state(0, index) if index < 4 else state(1, 0)
-            if name in ("u", "v"):
-                scale = wave.inverse_lap()
-                real, imag = real * scale, imag * scale
-            factor = {"u": wave.dy, "v": -wave.dx, "wx": wave.dx, "wy": wave.dy}[name]
-            reals.append(-imag * factor)
-            imags.append(real * factor)
+            real, imag = sources["psi" if name in ("u", "v") else "w", index]
+            factor = rows[index].slope if name in ("u", "wy") else across
+            if name == "v":
+                reals.append(imag * factor)
+                imags.append(-real * factor)
+            else:
+                reals.append(-imag * factor)
+                imags.append(real * factor)
         mine = lane_slot == place
         moved = roll(reals[4], 8 * place), roll(imags[4], 8 * place)
         last_real = jnp.where(mine, moved[0], 0.0 if last_real is None else last_real)
@@ -344,9 +383,11 @@
 
 
 FIRST = ("left", "forward_y", "turn_y", "low_rows", "turn_low")
-WAVES = ("left", "right_x", "turn_x")
-MIDDLE = ("left", "right_x", "turn_x", "half")
+WAVES = ("left", "right_x", "turn_x", "wave_x")
+MIDDLE = WAVES + ("half",)
+FINAL = WAVES + ("coarse_rows", "coarse_turn")
 ROWS = ("left", "forward_y", "inverse_y", "turn_y", "half")
+PRODUCT = ROWS + ("drive_spots",)
 LAST = ROWS + ("coarse_y", "coarse_x")
 
 
@@ -364,12 +405,23 @@
     return groups
 
 
-def first_kernel(vorticity_ref, forcing_ref, *rest):
-    tab = Tables(FIRST, rest)
-    out_ref = rest[len(FIRST)]
+def first_kernel(*rest):
+    total = 2 + len(FIRST)
+    out_ref, *held, ready = rest[total + 1 :]
+    copies = {}
+    for name in ("rows", "forward_y", "turn_y", "left", "force", "low_rows", "turn_low"):
+        k = ("rows", "force").index(name) if name in ("rows", "force") else 2 + FIRST.index(name)
+        copies[name] = pltpu.make_async_copy(rest[k], held[k], ready.at[k])
+        copies[name].start()
+    vorticity_ref, forcing_ref = held[:2]
+    tab = Tables(FIRST, held[2:])
+    for name in ("rows", "forward_y", "turn_y", "left"):
+        copies[name].wait()
     direct, mirror = y_forward(tab, grid_groups(vorticity_ref))
     store_set(out_ref, 0, 17, *direct)
     store_set(out_ref, 8, 17, *mirror)
+    for name in ("force", "low_rows", "turn_low"):
+        copies[name].wait()
     groups = grid_groups(forcing_ref)
     values = jnp.concatenate([g[k] for g in groups for k in range(2)], axis=1)
     high, low = halves(values)
@@ -390,10 +442,10 @@
     store(out_ref, 16, 17, packed)
 
 
-def start_kernel(scalars, in_ref, *rest):
+def start_kernel(in_ref, *rest):
     tab = Tables(WAVES, rest)
     state_ref, out_ref = rest[len(WAVES) :]
-    rank = scalars[0]
+    rank = rank_here()
     for group in range(2):
         real, imag = x_forward(tab, *load_set(in_ref, 8 * group, 17))
         for q in range(4):
@@ -425,7 +477,7 @@
     return y_inverse(tab, real, imag, last, place)
 
 
-def drive_rows(real, imag):
+def drive_rows(tab, real, imag):
     lane = lane_ids()
     columns = jnp.where(lane < 4, roll(real, -24), roll(imag, -20)).T
     pick = lambda index: jnp.broadcast_to(columns[index : index + 1, :], (8, 128))
@@ -439,14 +491,19 @@
         top = jnp.where(sub == k, plus[k], top)
         after = minus[k + 1] if k < 3 else 0.0
         bottom = jnp.where(sub == 7 - k, jnp.where(start, after, minus[k]), bottom)
-    return jnp.concatenate([top, jnp.zeros((112, 128), jnp.float32), bottom], axis=0)
+    spots = tab["drive_spots"]
+    made = []
+    for values, table in ((top, spots[:128]), (bottom, spots[128:])):
+        high, low = halves(values)
+        made.append(dot(high, table) + dot(low, table))
+    return jnp.concatenate([made[0], jnp.zeros((112, 128), jnp.float32), made[1]], axis=0)
 
 
 def product_first_kernel(in_ref, local_ref, *rest):
-    tab = Tables(ROWS, rest)
-    out_ref = rest[len(ROWS)]
+    tab = Tables(PRODUCT, rest)
+    out_ref = rest[len(PRODUCT)]
     last_real, last_imag = load(in_ref, 24, 26), load(in_ref, 25, 26)
-    store(out_ref, 16, 17, drive_rows(last_real, last_imag))
+    store(out_ref, 16, 17, drive_rows(tab, last_real, last_imag))
     last = last_row(tab, last_real, last_imag)
     u0, u1 = product_one(tab, in_ref, 26, last, 0)
     x0, x1 = product_one(tab, in_ref, 26, last, 2)
@@ -476,7 +533,7 @@
     store_set(out_ref, 8, 17, *mirror)
 
 
-def product_kernel(scalars, in_ref, *rest):
+def product_kernel(in_ref, *rest):
     tab = Tables(LAST, rest)
     out_ref, mixed_ref = rest[len(LAST) :]
     got = load(in_ref, 34, 35)
@@ -520,66 +577,77 @@
     for odd in range(2):
         for side in range(2):
             piece = share[128 * odd : 128 * odd + 128, 128 * side : 128 * side + 128]
-            piece = pltpu.roll(piece, scalars[0], 0)
+            piece = pltpu.roll(piece, rank_here(), 0)
             store(out_ref, 16 + 2 * odd + side, 20, piece)
 
 
-def drive_blocks(rank, values):
-    shape = (128, 128)
-    source = row_ids()
+def shelled(rank, values, radii):
     lane = lane_ids()
-    number = 8 * (lane >> 5) + (lane & 7)
-    side = jnp.where(number == 0, 0, jnp.where(number == 31, 1, 4))
-    made = []
-    for group in range(2):
-        for q in range(4):
-            slot = 4 * q + ((lane >> 3) & 3)
-            back = jnp.where(slot == 0, 16 * group, 32 - slot)
-            near, far = (slot, back) if group == 0 else (back, jnp.where(slot == 0, 16, slot))
-            slot = jnp.where(rank < 64, near, far)
-            for part in range(2):
-                want = 64 * part + 32 * side + slot
-                want = jnp.where(side == 4, -1, want)
-                made.append(jnp.where(source == want, 1.0, 0.0).astype(jnp.bfloat16))
-    select = jnp.concatenate(made, axis=1)
-    high, low = halves(values)
-    out = dot(
-        jnp.concatenate([high, low], axis=1), jnp.concatenate([select, select], axis=0)
-    )
-    return lambda place: out[:, 128 * place : 128 * place + 128]
-
-
-def middle_kernel(scalars, in_ref, state_ref, *rest):
+    side, spot = (lane >> 5) & 1, lane & 7
+    slot = 4 * (spot & 3) + ((lane >> 3) & 3)
+    slot = jnp.where(spot < 4, slot, jnp.where(slot == 0, 16, 32 - slot))
+    my = 32 * rank + slot
+    my = jnp.where(my < GRID // 2, my, my - GRID)
+    mx = row_ids() - 128 * side
+    squares = mx * mx + my * my
+    mask = None
+    for radius in radii:
+        inside = (radius * radius <= squares) & (squares < (radius + 1) * (radius + 1))
+        mask = inside if mask is None else mask | inside
+    return jnp.where(mask, values, 0.0)
+
+
+def fetch(ready, pairs):
+    copies = [
+        pltpu.make_async_copy(source, target, ready.at[k])
+        for k, (source, target) in enumerate(pairs)
+    ]
+    for copy in copies:
+        copy.start()
+    return copies
+
+
+def middle_kernel(cutoff_from, shells_from, in_ref, state_ref, *rest):
     tab = Tables(MIDDLE, rest)
-    ahead_ref, out_ref, next_ref = rest[len(MIDDLE) :]
-    rank, cutoff = scalars[0], scalars[1]
-    radii = [scalars[2 + k] for k in range(SHELLS)]
+    ahead_ref, out_ref, next_ref, cutoff_ref, shells_ref, ready = rest[len(MIDDLE) :]
+    copies = fetch(ready, ((cutoff_from, cutoff_ref), (shells_from, shells_ref)))
+    rank = rank_here()
     lane = lane_ids()
-    drive_of = drive_blocks(rank, load(in_ref, 16, 17))
+    spectra = [x_forward(tab, *load_set(in_ref, 8 * group, 17)) for group in range(2)]
+    for copy in copies:
+        copy.wait()
+    cutoff = cutoff_ref[0]
+    forcing = shelled(rank, load(in_ref, 16, 17), [shells_ref[k] for k in range(SHELLS)])
+    first_spots = (lane < 32) & ((lane & 7) == 0)
+    last_spots = (lane >= 96) & ((lane & 7) == 7)
+    keep_x = keep_columns(tab, cutoff)
+    squares, low_x = tab.turn("wave_x", 1), tab.turn("wave_x", 2)
     low0 = [0.0, 0.0]
     low1 = [0.0, 0.0]
     for group in range(2):
-        real, imag = x_forward(tab, *load_set(in_ref, 8 * group, 17))
+        real, imag = spectra[group]
         for q in range(4):
-            wave = Waves(rank, group, q)
-            keep = wave.keep(cutoff)
-            shell = wave.shell(radii)
-            low = wave.low()
-            damp = viscosity * wave.lap
+            rows = Rows(rank, group, q)
+            keep = keep_x * rows.keep(cutoff)
+            low = low_x * rows.low()
+            damp = (viscosity * unit * unit) * (squares + rows.square)
             spot = 4 * group + q
             mine = (lane < 32) & ((lane & 7) == spot)
             for part, term in enumerate((real[q], imag[q])):
                 place = 8 * group + 2 * q + part
                 now = block(state_ref, place)
-                drive = jnp.where(shell, drive_of(place), 0.0)
-                slope = drive - jnp.where(keep, term, 0.0) - damp * now
+                drive = jnp.where(first_spots, roll(forcing, -64 * part - spot), 0.0)
+                drive = jnp.where(
+                    last_spots, roll(forcing, 71 - 64 * part - spot), drive
+                )
+                slope = drive - keep * term - damp * now
                 after = now + time_step * slope
                 put(next_ref, place, after)
                 rest_slope = slope + drive - damp * after
-                done = now + 0.5 * time_step * rest_slope
-                lifted = jnp.where(low, done + coarse_ratio * (done - now), done)
+                change = 0.5 * time_step * rest_slope
+                lifted = now + change + (coarse_ratio * low) * change
                 put(ahead_ref, place, lifted)
-                lifted = jnp.where(low, lifted, 0.0)
+                lifted = low * lifted
                 low0[part] = jnp.where(mine, roll(lifted, spot), low0[part])
                 low1[part] = jnp.where(mine, roll(lifted, 25 + spot), low1[part])
     even = [a + b for a, b in zip(low0, low1)]
@@ -597,21 +665,23 @@
     send_fields(tab, rank, state, out_ref, 35, ("u", "v", "wx", "wy"))
 
 
-def final_kernel(scalars, in_ref, ahead_ref, coarse_ref, *rest):
-    tab = Tables(WAVES, rest)
-    out_ref, points_ref = rest[len(WAVES) :]
-    rank, cutoff = scalars[0], scalars[1]
-    for odd in range(2):
-        for side in range(2):
-            total = jnp.sum(load(in_ref, 16 + 2 * odd + side, 20), axis=0, keepdims=True)
-            at = slice(128 * side, 128 * side + 128)
-            points_ref[odd : odd + 1, at] = coarse_ref[odd : odd + 1, at] + total
+def final_kernel(cutoff_from, in_ref, ahead_ref, mixed_ref, *rest):
+    tab = Tables(FINAL, rest)
+    out_ref, points_ref, held_ref, cutoff_ref, ready, done_ref = rest[len(FINAL) :]
+    (copy,) = fetch(ready, ((cutoff_from, cutoff_ref),))
+    rank = rank_here()
+    spectra = [x_forward(tab, *load_set(in_ref, 8 * group, 20)) for group in range(2)]
+    copy.wait()
+    cutoff = cutoff_ref[0]
+    keep_x = keep_columns(tab, cutoff) * (0.5 * time_step)
+    low_x = tab.turn("wave_x", 2) * coarse_ratio
+    copies = []
     for group in range(2):
-        real, imag = x_forward(tab, *load_set(in_ref, 8 * group, 20))
+        real, imag = spectra[group]
         for q in range(4):
-            wave = Waves(rank, group, q)
-            factor = jnp.where(wave.low(), (1 + coarse_ratio) * 0.5 * time_step, 0.5 * time_step)
-            factor = jnp.where(wave.keep(cutoff), factor, 0.0)
+            rows = Rows(rank, group, q)
+            factor = keep_x * rows.keep(cutoff)
+            factor = factor + factor * (low_x * rows.low())
             for part, term in enumerate((real[q], imag[q])):
                 lifted = block(ahead_ref, 8 * group + 2 * q + part) - factor * term
                 flipped = lifted.T
@@ -624,24 +694,56 @@
                             number = 16 if number == 0 else 32 - number
                         for kl in range(8):
                             col = 128 * (8 * kh + kl)
-                            out_ref[part, number, col : col + 128] = piece[kl]
+                            held_ref[part, number, col : col + 128] = piece[kl]
+        for part in range(2):
+            spot = (part, slice(16 * group, 16 * group + 16))
+            copies.append(
+                pltpu.make_async_copy(
+                    held_ref.at[spot], out_ref.at[spot], done_ref.at[2 * group + part]
+                )
+            )
+            copies[-1].start()
+    mixed = mixed_ref[...]
+    high, low = halves(jnp.concatenate([mixed, roll(mixed, -32)], axis=0))
+    out = dot(
+        jnp.concatenate([high, low, high], axis=1), thrice(tab["coarse_rows"], 0)
+    )
+    turn = tab["coarse_turn"]
+    for odd in range(2):
+        rows = out[8 * odd : 8 * odd + 8]
+        rows = rows[:, :LOW] * turn[:8] + rows[:, LOW:] * turn[8:]
+        line = jnp.sum(rows, axis=0, keepdims=True)
+        for side in range(2):
+            total = jnp.sum(load(in_ref, 16 + 2 * odd + side, 20), axis=0, keepdims=True)
+            at = slice(128 * side, 128 * side + 128)
+            points_ref[odd : odd + 1, at] = line[:, at] + total
+    for copy in copies:
+        copy.wait()
 
 
 VMEM = pl.BlockSpec(memory_space=pltpu.VMEM)
-SMEM = pl.BlockSpec(memory_space=pltpu.SMEM)
-
-
-def call(kernel, name, outs, args, scalar=False):
-    specs = [SMEM] if scalar else []
-    specs = specs + [VMEM] * (len(args) - len(specs))
+
+
+HBM = pl.BlockSpec(memory_space=pltpu.HBM)
+
+
+def call(kernel, name, outs, args, far=(), out_specs=None, scratch=()):
+    far = tuple(
+        a if a.ndim == 1 else pltpu.with_memory_space_constraint(a, pltpu.HBM) for a in far
+    )
     return pl.pallas_call(
         kernel,
         name=name,
         out_shape=[jax.ShapeDtypeStruct(shape, jnp.float32) for shape in outs],
-        in_specs=specs,
-        out_specs=[VMEM] * len(outs),
+        in_specs=[HBM] * len(far) + [VMEM] * len(args),
+        out_specs=out_specs or [VMEM] * len(outs),
+        scratch_shapes=list(scratch),
         compiler_params=pltpu.CompilerParams(vmem_limit_bytes=VMEM_LIMIT * 1024 * 1024),
-    )(*args)
+    )(*far, *args)
+
+
+def near(array):
+    return pltpu.with_memory_space_constraint(array, pltpu.VMEM)
 
 
 def exchange(buffer, count):
@@ -650,64 +752,60 @@
     return cut.reshape(128 * count, 128)
 
 
-@functools.lru_cache(None)
-def coarse_table():
-    source = np.array([0, 1, 2, 3, 124, 125, 126, 127])
-    slot = np.arange(32)
-    inner, spot = slot >> 3, slot & 7
-    number = 4 * (spot & 3) + inner
-    row = np.where(spot < 4, number, np.where(number == 0, 16, 32 - number))
-    wave = 32 * source[:, None] + row[None, :]
-    angle = 2 * np.pi * ((wave[:, :, None] * np.arange(LOW)) % LOW) / LOW
-    return (np.stack([np.cos(angle), -np.sin(angle)], axis=1) * (8 / LOW)).astype(np.float32)
-
-
 def body(vorticity_grid, forcing_grid, cutoff, forcing_shells):
-    rank = lax.axis_index("gx") * lax.axis_size("gy") + lax.axis_index("gy")
-    scalars = jnp.concatenate([rank[None].astype(jnp.int32), cutoff, forcing_shells])
     made = {name: jnp.asarray(table) for name, table in tables().items()}
     tabs = lambda names: tuple(made[name] for name in names)
     spectrum = (16 * 128, 128)
+    args = (vorticity_grid, forcing_grid) + tabs(FIRST)
     (sent,) = call(
-        first_kernel, "first", [(128 * 17, 128)], (vorticity_grid, forcing_grid) + tabs(FIRST)
+        first_kernel,
+        "first",
+        [(128 * 17, 128)],
+        (),
+        args + (cutoff,),
+        scratch=[pltpu.VMEM(a.shape, a.dtype) for a in args]
+        + [pltpu.SemaphoreType.DMA((len(args),))],
     )
     got = exchange(sent, 17)
     state, fields = call(
-        start_kernel, "start", [spectrum, (128 * 26, 128)], (scalars, got) + tabs(WAVES), True
+        start_kernel, "start", [spectrum, (128 * 26, 128)], (got,) + tabs(WAVES)
     )
     got = exchange(fields, 26)
     (term,) = call(
-        product_first_kernel, "product_first", [(128 * 17, 128)], (got, sent) + tabs(ROWS)
+        product_first_kernel, "product_first", [(128 * 17, 128)], (got, near(sent)) + tabs(PRODUCT)
     )
     got = exchange(term, 17)
-    ahead, fields, _ = call(
+    ahead, fields = call(
         middle_kernel,
         "middle",
-        [spectrum, (128 * 35, 128), spectrum],
-        (scalars, got, state) + tabs(MIDDLE),
-        True,
+        [spectrum, (128 * 35, 128)],
+        (got, near(state)) + tabs(MIDDLE),
+        (cutoff, forcing_shells),
+        scratch=[
+            pltpu.VMEM(spectrum, jnp.float32),
+            pltpu.SMEM((1,), jnp.int32),
+            pltpu.SMEM((SHELLS,), jnp.int32),
+            pltpu.SemaphoreType.DMA((2,)),
+        ],
     )
     got = exchange(fields, 35)
     term, mixed = call(
-        product_kernel,
-        "product",
-        [(128 * 20, 128), (8, 128)],
-        (scalars, got) + tabs(LAST),
-        True,
+        product_kernel, "product", [(128 * 20, 128), (8, 128)], (got,) + tabs(LAST)
     )
     got = exchange(term, 20)
-    coarse = jnp.einsum(
-        "sceq,scqb->eb",
-        mixed.reshape(8, 2, 2, 32),
-        jnp.asarray(coarse_table()),
-        precision=lax.Precision.HIGHEST,
-    )
     lifted, coarse = call(
         final_kernel,
         "final",
         [(2, 32, GRID), (2, LOW)],
-        (scalars, got, ahead, coarse) + tabs(WAVES),
-        True,
+        (got, near(ahead), mixed) + tabs(FINAL),
+        (cutoff,),
+        out_specs=[HBM, VMEM],
+        scratch=[
+            pltpu.VMEM((2, 32, GRID), jnp.float32),
+            pltpu.SMEM((1,), jnp.int32),
+            pltpu.SemaphoreType.DMA((1,)),
+            pltpu.SemaphoreType.DMA((4,)),
+        ],
     )
     return lifted, coarse
 

time: 183 us -> 175 us (0.956)
  blocking collectives: 89.7 us -> 147 us
  waiting for transfers between devices: 40.6 us -> 0 us
  starting transfers between devices: 15.2 us -> 0 us
  local copies, waits for them, and re-layouts: 7.48 us -> 0.1 us
    all_to_all x3 -> x5, blocking collectives: 89.7 us -> 147 us  [exchange(): cut = lax.all_to_all(cut, AXES, split_axis=0, concat_axis=0, tiled=True)]
    all_to_all x2 -> x0, waiting for transfers between devices: 40.6 us -> none  [exchange(): cut = lax.all_to_all(cut, AXES, split_axis=0, concat_axis=0, tiled=True)]
    all_to_all x2 -> x0, starting transfers between devices: 15.2 us -> none  [exchange(): cut = lax.all_to_all(cut, AXES, split_axis=0, concat_axis=0, tiled=True)]
    unnamed x36 -> x28, local copies, waits for them, and re-layouts: 6.79 us -> 0.1 us
  transfers between devices with their start and end apart: 2 -> 0, of which waited for: 2 -> 0; matrix products, arithmetic and copies ran while one was open for 1% -> 0% of each run, Pallas kernels for 0% -> 0%
where the time goes in v2:
time: 175 us
  blocking collectives  147 us (84%)
  Pallas kernels  25.8 us (15%)
    all_to_all x5, blocking collectives, exchange(): cut = lax.all_to_all(cut, AXES, split_axis=0, concat_axis=0, tiled=True)  147 us
    pallas_call x6, Pallas kernels, call(): pl.pallas_call(kernel, name=name, out_shape=[jax.ShapeDtypeStruct(shape,...  25.8 us

profile of v2, /device:TPU:1, one launch (start us, length us, event | category | flops | bytes accessed | tf_op | source)
XLA Modules:
  0.0 174.7 jit_solution(8923131124672567572)
XLA Ops:
  1.3 3.7 %first.1.local_ref = f32[2176,128]{1,0:T(8,128)S(1)} custom-call(f32[32,4096]{1,0:T(8,128)} %rest_0_.6, f32[32,4096]{1,0:T(8,128)} %rest_1_.6, bf16[256,512]{1,0:T(8,128)(2,1)} %constant.30.clone.rest_2_.rest_0_, bf16[512,256]{1,0:T(8,128)(2,1)} %constant.32.clone.rest_3_.rest_1_, f32[512,128]{1,0:T(8,128)} %constant.35.clone.rest_4_.rest_3_, ...), custom_call_target="tpu_custom_call" | custom-call | tf_op jit(solution)/shard_map/first/pallas_call | solution.py:734
  5.0 0.0 copy-start
  5.0 0.0 copy-start.1
  5.0 0.0 copy-start.4
  5.0 0.0 copy-start.6
  5.0 31.7 %all_to_all.25 = f32[128,1,2176]{2,1,0:T(1,128)S(1)} all-to-all(f32[128,1,2176]{2,1,0:T(1,128)S(1)} %bitcast.10), channel_id=1, replica_groups=mesh['gx'=32,'gy'=4] {'gx','gy'}, dimensions={0} | all-to-all | bytes 2228224 | tf_op jit(solution)/shard_map/all_to_all | solution.py:751
  36.7 0.0 copy-done
  36.7 0.0 copy-done.1
  36.8 0.0 copy-done.4
  36.8 0.0 copy-done.6
  36.8 3.6 %start.1 = (f32[2048,128]{1,0:T(8,128)S(1)}, f32[3328,128]{1,0:T(8,128)S(1)}) custom-call(f32[2176,128]{1,0:T(8,128)S(1)} %bitcast.15, bf16[256,512]{1,0:T(8,128)(2,1)S(1)} %copy-done, bf16[512,256]{1,0:T(8,128)(2,1)S(1)} %copy-done.1, f32[256,128]{1,0:T(8,128)S(1)} %copy-done.6, f32[384,128]{1,0:T(8,128)S(1)} %copy-done.4), custom_call_target="tpu_custom_call" | custom-call | tf_op jit(solution)/shard_map/start/pallas_call | solution.py:734
  40.4 0.0 copy-start.2
  40.4 0.0 copy-start.3
  40.4 0.0 copy-start.5
  40.4 0.0 copy-start.7
  40.5 0.0 copy-start.11
  40.5 30.0 %all_to_all.26 = f32[128,1,3328]{2,1,0:T(1,128)S(1)} all-to-all(f32[128,1,3328]{2,1,0:T(1,128)S(1)} %bitcast.18), channel_id=1, replica_groups=mesh['gx'=32,'gy'=4] {'gx','gy'}, dimensions={0} | all-to-all | bytes 3407872 | tf_op jit(solution)/shard_map/all_to_all | solution.py:751
  70.4 0.0 copy-done.3
  70.5 4.0 %product_first.1 = f32[2176,128]{1,0:T(8,128)S(1)} custom-call(f32[3328,128]{1,0:T(8,128)S(1)} %bitcast.12, f32[2176,128]{1,0:T(8,128)S(1)} %first.1.local_ref, bf16[256,512]{1,0:T(8,128)(2,1)S(1)} %copy-done, bf16[512,256]{1,0:T(8,128)(2,1)S(1)} %copy-done.3, bf16[512,256]{1,0:T(8,128)(2,1)S(1)} %copy-done.7, f32[512,128]{1,0:T(8,128)S(1)} %copy-done.2, ...), custom_call_target="tpu_custom_call" | custom-call | tf_op jit(solution)/shard_map/product_first/pallas_call | solution.py:734
  74.5 0.0 copy-start.13
  74.5 23.5 %all_to_all.27 = f32[128,1,2176]{2,1,0:T(1,128)S(1)} all-to-all(f32[128,1,2176]{2,1,0:T(1,128)S(1)} %bitcast.14), channel_id=1, replica_groups=mesh['gx'=32,'gy'=4] {'gx','gy'}, dimensions={0} | all-to-all | bytes 2228224 | tf_op jit(solution)/shard_map/all_to_all | solution.py:751
  98.0 0.0 copy-done.13
  98.0 6.2 %middle.1 = (f32[2048,128]{1,0:T(8,128)S(1)}, f32[4480,128]{1,0:T(8,128)S(1)}) custom-call(s32[1]{0:T(128)S(6)} %copy.26.rest_7_.cutoff_from, s32[4]{0:T(128)S(1)} %copy-done.13, f32[2176,128]{1,0:T(8,128)S(1)} %bitcast.16, f32[2048,128]{1,0:T(8,128)S(1)} %get-tuple-element.9.state_ref, bf16[256,512]{1,0:T(8,128)(2,1)S(1)} %copy-done, ...), custom_call_target="tpu_custom_call" | custom-call | tf_op jit(solution)/shard_map/middle/pallas_call | solution.py:734
  104.2 0.0 copy-start.8
  104.3 0.0 copy-start.10
  104.3 36.3 %all_to_all.28 = f32[128,1,4480]{2,1,0:T(1,128)S(1)} all-to-all(f32[128,1,4480]{2,1,0:T(1,128)S(1)} %bitcast.17), channel_id=1, replica_groups=mesh['gx'=32,'gy'=4] {'gx','gy'}, dimensions={0} | all-to-all | bytes 4587520 | tf_op jit(solution)/shard_map/all_to_all | solution.py:751
  140.5 0.0 copy-done.10
  140.6 4.1 %product.1 = (f32[2560,128]{1,0:T(8,128)S(1)}, f32[8,128]{1,0:T(8,128)S(1)}) custom-call(f32[4480,128]{1,0:T(8,128)S(1)} %bitcast.11, bf16[256,512]{1,0:T(8,128)(2,1)S(1)} %copy-done, bf16[512,256]{1,0:T(8,128)(2,1)S(1)} %copy-done.3, bf16[512,256]{1,0:T(8,128)(2,1)S(1)} %copy-done.7, f32[512,128]{1,0:T(8,128)S(1)} %copy-done.2, f32[256,128]{1,0:T(8,128)S(1)} %copy-done.5, ...), custom_call_target="tpu_custom_call" | custom-call | tf_op jit(solution)/shard_map/product/pallas_call | solution.py:734
  144.7 0.0 copy-start.9
  144.7 0.0 copy-start.12
  144.7 25.7 %all_to_all.29 = f32[128,1,2560]{2,1,0:T(1,128)S(1)} all-to-all(f32[128,1,2560]{2,1,0:T(1,128)S(1)} %bitcast.19), channel_id=1, replica_groups=mesh['gx'=32,'gy'=4] {'gx','gy'}, dimensions={0} | all-to-all | bytes 2621440 | tf_op jit(solution)/shard_map/all_to_all | solution.py:751
  170.4 4.1 %final.1 = (f32[2,32,4096]{2,1,0:T(8,128)}, f32[2,256]{1,0:T(2,128)}) custom-call(s32[1]{0:T(128)S(6)} %copy.26.rest_7_.cutoff_from, f32[2560,128]{1,0:T(8,128)S(1)} %bitcast.13, f32[2048,128]{1,0:T(8,128)S(1)} %get-tuple-element.12.ahead_ref, f32[8,128]{1,0:T(8,128)S(1)} %get-tuple-element.13.mixed_ref, bf16[256,512]{1,0:T(8,128)(2,1)S(1)} %copy-done, ...), custom_call_target="tpu_custom_call" | custom-call | tf_op jit(solution)/shard_map/final/pallas_call | solution.py:734
  (7 shorter events, 0.0 us)
Async XLA Ops:
  5.0 31.8 %copy-start = (bf16[256,512]{1,0:T(8,128)(2,1)S(1)}, bf16[256,512]{1,0:T(8,128)(2,1)}, u32[]{:S(2)}) copy-start(bf16[256,512]{1,0:T(8,128)(2,1)} %constant.30.clone.rest_2_.rest_0_) | copy-start | bytes 786436
  5.0 31.8 %copy-start.1 = (bf16[512,256]{1,0:T(8,128)(2,1)S(1)}, bf16[512,256]{1,0:T(8,128)(2,1)}, u32[]{:S(2)}) copy-start(bf16[512,256]{1,0:T(8,128)(2,1)} %constant.31.clone.rest_1_) | copy-start | bytes 786436
  5.0 31.8 %copy-start.4 = (f32[384,128]{1,0:T(8,128)S(1)}, f32[384,128]{1,0:T(8,128)}, u32[]{:S(2)}) copy-start(f32[384,128]{1,0:T(8,128)} %constant.37.clone.rest_3_) | copy-start | bytes 589828
  5.0 31.8 %copy-start.6 = (f32[256,128]{1,0:T(8,128)S(1)}, f32[256,128]{1,0:T(8,128)}, u32[]{:S(2)}) copy-start(f32[256,128]{1,0:T(8,128)} %constant.34.clone.rest_2_) | copy-start | bytes 393220
  40.4 30.0 %copy-start.2 = (f32[512,128]{1,0:T(8,128)S(1)}, f32[512,128]{1,0:T(8,128)}, u32[]{:S(2)}) copy-start(f32[512,128]{1,0:T(8,128)} %constant.35.clone.rest_4_.rest_3_) | copy-start | bytes 786436
  40.4 30.0 %copy-start.3 = (bf16[512,256]{1,0:T(8,128)(2,1)S(1)}, bf16[512,256]{1,0:T(8,128)(2,1)}, u32[]{:S(2)}) copy-start(bf16[512,256]{1,0:T(8,128)(2,1)} %constant.32.clone.rest_3_.rest_1_) | copy-start | bytes 786436
  40.4 30.0 %copy-start.5 = (f32[256,128]{1,0:T(8,128)S(1)}, f32[256,128]{1,0:T(8,128)}, u32[]{:S(2)}) copy-start(f32[256,128]{1,0:T(8,128)} %constant.36.clone.rest_4_) | copy-start | bytes 393220
  40.4 30.0 %copy-start.7 = (bf16[512,256]{1,0:T(8,128)(2,1)S(1)}, bf16[512,256]{1,0:T(8,128)(2,1)}, u32[]{:S(2)}) copy-start(bf16[512,256]{1,0:T(8,128)(2,1)} %constant.33.clone.rest_2_) | copy-start | bytes 786436
  40.5 30.0 %copy-start.11 = (bf16[256,128]{1,0:T(8,128)(2,1)S(1)}, bf16[256,128]{1,0:T(8,128)(2,1)}, u32[]{:S(2)}) copy-start(bf16[256,128]{1,0:T(8,128)(2,1)} %constant.38.clone.rest_5_) | copy-start | bytes 196612
  74.5 23.5 %copy-start.13 = (s32[4]{0:T(128)S(1)}, s32[4]{0:T(128)}, u32[]{:S(2)}) copy-start(s32[4]{0:T(128)} %shells_from.1) | copy-start | bytes 52
  104.2 36.3 %copy-start.8 = (bf16[1024,256]{1,0:T(8,128)(2,1)S(1)}, bf16[1024,256]{1,0:T(8,128)(2,1)}, u32[]{:S(2)}) copy-start(bf16[1024,256]{1,0:T(8,128)(2,1)} %constant.43.clone.rest_5_) | copy-start | bytes 1572868
  104.3 36.3 %copy-start.10 = (bf16[256,256]{1,0:T(8,128)(2,1)S(1)}, bf16[256,256]{1,0:T(8,128)(2,1)}, u32[]{:S(2)}) copy-start(bf16[256,256]{1,0:T(8,128)(2,1)} %constant.44.clone.rest_6_) | copy-start | bytes 393220
  144.7 25.8 %copy-start.9 = (bf16[256,512]{1,0:T(8,128)(2,1)S(1)}, bf16[256,512]{1,0:T(8,128)(2,1)}, u32[]{:S(2)}) copy-start(bf16[256,512]{1,0:T(8,128)(2,1)} %constant.39.clone.rest_4_) | copy-start | bytes 786436
  144.7 25.8 %copy-start.12 = (f32[16,256]{1,0:T(8,128)S(1)}, f32[16,256]{1,0:T(8,128)}, u32[]{:S(2)}) copy-start(f32[16,256]{1,0:T(8,128)} %constant.40.clone.rest_5_) | copy-start | bytes 49156

commit v3 on v2

--- a/solution.py
+++ b/solution.py
@@ -36,6 +36,15 @@
     angle = 2 * np.pi * np.outer(index, index) / 128
     cos, sin = np.cos(angle) / 8, np.sin(angle) / 8
     made["left"] = split_np(np.block([[cos, sin], [-sin, cos]]), 1)
+
+    near = (index >= 1) & (index < 64)
+    far = index >= 64
+    angle = 2 * np.pi * np.outer(index, index) / 128
+    later = 2 * np.pi * np.outer(index, index + 0.5) / 128
+    real = np.where(near, 2 * np.cos(angle), np.where(index == 0, 1.0, 0.0))
+    imag = np.where(near, -2 * np.sin(angle), np.where(index == 0, (-1.0) ** rows, 0.0))
+    edge = [[real, imag], [far * 2 * np.cos(later), far * -2 * np.sin(later)]]
+    made["left_edge"] = split_np(np.block(edge) / 8, 1)
 
     lane = np.arange(128)
     inner = 8 * (lane >> 5) + (lane & 7)
@@ -105,6 +114,13 @@
     source = np.array([0, 1, 2, 3, 124, 125, 126, 127])[:, None]
     angle = 2 * np.pi * (source * point % 8) / 8
     made["coarse_turn"] = planes([np.cos(angle), -np.sin(angle)])
+
+    flips = [
+        (slot[:, None] == slot[None, :]) & (inner[:, None] == want[None, :])
+        for want in (31 - inner, (32 - inner) % 32)
+    ]
+    flips.append(rows == (128 - index[None, :]) % 128)
+    made["flip"] = np.concatenate(flips, axis=0).astype(np.float32).astype(jnp.bfloat16)
 
     angle = 2 * np.pi * np.outer(index, index) / GRID
     low = np.concatenate([np.cos(angle), -np.sin(angle)], axis=0) / 64
@@ -269,23 +285,31 @@
     return direct, mirror
 
 
-def y_inverse(tab, real, imag, last, place):
+def y_inverse(tab, real, imag, edge, place):
     imag, real = left_many(tab["left"], imag, real)
     start = lane_ids() < 8
-    cos, sin = tab.turn("turn_y", 0), tab.turn("turn_y", 1)
-    cos = jnp.where(start, cos, 2.0 * cos)
-    sin = 2.0 * sin
-    part0 = [p * cos - q * sin for p, q in zip(real, imag)]
-    part1 = [p * sin + q * cos for p, q in zip(real, imag)]
-    part1 = [
-        jnp.where(start, roll(last, -(32 * xh + 8 * place)), part1[xh]) for xh in range(4)
+    cos, sin = 2.0 * tab.turn("turn_y", 0), 2.0 * tab.turn("turn_y", 1)
+    parts = [
+        [p * cos - q * sin for p, q in zip(real, imag)],
+        [p * sin + q * cos for p, q in zip(real, imag)],
     ]
-    return right_many(tab["inverse_y"], part0, part1)
-
-
-def last_row(tab, real, imag):
-    imag, real = left_many(tab["left"], [imag], [real])
-    return real[0] * tab.turn("half", 0) - imag[0] * tab.turn("half", 1)
+    for part, values in zip(parts, edge):
+        for xh in range(4):
+            part[xh] = jnp.where(start, roll(values, -(32 * xh + 8 * place)), part[xh])
+    return right_many(tab["inverse_y"], *parts)
+
+
+def edge_rows(tab, sets):
+    lane = lane_ids()
+    packed = [0.0, 0.0]
+    for place, both in enumerate(sets):
+        for part, blocks in enumerate(both):
+            for xh in range(4):
+                mine = (lane >> 3) == 4 * xh + place
+                moved = roll(blocks[xh], 32 * xh + 8 * place)
+                packed[part] = jnp.where(mine, moved, packed[part])
+    first, second = left_many(tab["left_edge"], [packed[0]], [packed[1]])
+    return first[0], second[0]
 
 
 def load(ref, index, count):
@@ -326,6 +350,8 @@
         slot = 4 * quarter + ((lane >> 3) & 3)
         if group == 1:
             slot = jnp.where(slot == 0, 16, 32 - slot)
+        if group == 2:
+            slot = jnp.where((slot == 0) & (rank >= 64), 16, slot)
         row = 32 * rank + slot
         my = jnp.where(row < GRID // 2, row, row - GRID)
         self.my = my
@@ -344,22 +370,25 @@
     return jnp.where(tab.turn("wave_x", 1) <= (cutoff * cutoff).astype(jnp.float32), 1.0, 0.0)
 
 
-def send_fields(tab, rank, state, out_ref, count, names, extra=None):
-    total = len(names)
-    last_real, last_imag = None, None
-    lane_slot = (lane_ids() >> 3) & 3
-    rows = [Rows(rank, 0, q) for q in range(4)] + [Rows(rank, 1, 0)]
+def send_fields(tab, rank, state, hidden, out_ref, count, names):
+    rows = [Rows(rank, 2, q) for q in range(4)]
     across, squares = tab.turn("wave_x", 0), tab.turn("wave_x", 1)
     sources = {}
-    for index in range(5):
-        real, imag = state(0, index) if index < 4 else state(1, 0)
+    for index in range(4):
+        real, imag = state(0, index)
+        if index == 0:
+            upper = first_slot() & (rank >= 64)
+            real, imag = [
+                jnp.where(upper, other, own) for own, other in zip((real, imag), state(1, 0))
+            ]
         both = squares + rows[index].square
         scale = jnp.where(both == 0.0, 0.0, (1.0 / (unit * unit)) / jnp.maximum(both, 1.0))
         sources["w", index] = real, imag
         sources["psi", index] = real * scale, imag * scale
+    scale = (1.0 / (unit * unit)) / (squares + float((GRID // 2) ** 2))
     for place, name in enumerate(names):
         reals, imags = [], []
-        for index in range(5):
+        for index in range(4):
             real, imag = sources["psi" if name in ("u", "v") else "w", index]
             factor = rows[index].slope if name in ("u", "wy") else across
             if name == "v":
@@ -368,25 +397,50 @@
             else:
                 reals.append(-imag * factor)
                 imags.append(real * factor)
-        mine = lane_slot == place
-        moved = roll(reals[4], 8 * place), roll(imags[4], 8 * place)
-        last_real = jnp.where(mine, moved[0], 0.0 if last_real is None else last_real)
-        last_imag = jnp.where(mine, moved[1], 0.0 if last_imag is None else last_imag)
-        real, imag = x_inverse(tab, reals[:4], imags[:4])
+        if name in ("v", "wx"):
+            factor = across * scale if name == "v" else -across
+            reals[0] = reals[0] + hidden[0] * factor
+            imags[0] = imags[0] + hidden[1] * factor
+        real, imag = x_inverse(tab, reals, imags)
         store_set(out_ref, 8 * place, count, swap4(real), swap4(imag))
-    real, imag = x_inverse(tab, [last_real], [last_imag])
-    real, imag = real[0], imag[0]
-    if extra is not None:
-        real, imag = extra(real, 0), extra(imag, 1)
-    store(out_ref, 8 * total, count, real)
-    store(out_ref, 8 * total + 1, count, imag)
+
+
+def first_slot():
+    return ((lane_ids() >> 3) & 3) == 0
+
+
+def split_rows(tab, rank, real, imag):
+    flip = tab["flip"]
+    sub = row_ids()
+    both = jnp.concatenate([real, imag], axis=0)
+    high, low = halves(both)
+    pair = jnp.concatenate([high, low], axis=1)
+    twice = lambda table, axis: jnp.concatenate([table, table], axis=axis)
+    most = dot(pair, twice(flip[:128], 0))
+    top = dot(pair, twice(flip[128:256], 0))
+    wide = jnp.concatenate([most[:128], most[128:]], axis=1)
+    high, low = halves(wide)
+    wide = dot(twice(flip[256:], 1), jnp.concatenate([high, low], axis=0))
+    real_back = jnp.where(sub == 0, top[:128], wide[:, :128])
+    imag_back = jnp.where(sub == 0, top[128:], wide[:, 128:])
+    mine = first_slot() & (rank == 0)
+    own = [
+        jnp.where(mine, 0.5 * (real + real_back), real),
+        jnp.where(mine, 0.5 * (imag - imag_back), imag),
+    ]
+    hidden = [
+        jnp.where(mine, 0.5 * (imag + imag_back), 0.0),
+        jnp.where(mine, 0.5 * (real_back - real), 0.0),
+    ]
+    return own, hidden
 
 
 FIRST = ("left", "forward_y", "turn_y", "low_rows", "turn_low")
 WAVES = ("left", "right_x", "turn_x", "wave_x")
+START = WAVES + ("flip",)
 MIDDLE = WAVES + ("half",)
 FINAL = WAVES + ("coarse_rows", "coarse_turn")
-ROWS = ("left", "forward_y", "inverse_y", "turn_y", "half")
+ROWS = ("left", "left_edge", "forward_y", "inverse_y", "turn_y")
 PRODUCT = ROWS + ("drive_spots",)
 LAST = ROWS + ("coarse_y", "coarse_x")
 
@@ -418,7 +472,14 @@
     for name in ("rows", "forward_y", "turn_y", "left"):
         copies[name].wait()
     direct, mirror = y_forward(tab, grid_groups(vorticity_ref))
-    store_set(out_ref, 0, 17, *direct)
+    lane, row = lane_ids(), row_ids()
+    spot = (lane < 8) & (row == 0)
+    real, imag = direct
+    imag = [
+        jnp.where(spot, jnp.broadcast_to(p[64:65, :], (128, 128)), q)
+        for p, q in zip(real, imag)
+    ]
+    store_set(out_ref, 0, 17, real, imag)
     store_set(out_ref, 8, 17, *mirror)
     for name in ("force", "low_rows", "turn_low"):
         copies[name].wait()
@@ -443,11 +504,15 @@
 
 
 def start_kernel(in_ref, *rest):
-    tab = Tables(WAVES, rest)
-    state_ref, out_ref = rest[len(WAVES) :]
+    tab = Tables(START, rest)
+    state_ref, out_ref = rest[len(START) :]
     rank = rank_here()
     for group in range(2):
         real, imag = x_forward(tab, *load_set(in_ref, 8 * group, 17))
+        if group == 0:
+            (real[0], imag[0]), hidden = split_rows(tab, rank, real[0], imag[0])
+            put(state_ref, 16, hidden[0])
+            put(state_ref, 17, hidden[1])
         for q in range(4):
             put(state_ref, 8 * group + 2 * q, real[q])
             put(state_ref, 8 * group + 2 * q + 1, imag[q])
@@ -458,28 +523,28 @@
     imag = jnp.where(part == 0, roll(row, -8), jnp.where(part == 1, -row, 0.0))
     real, imag = x_plain(tab, [real], [imag])
 
-    def extra(values, which):
-        source = (real, imag)[which][0]
+    packed = jnp.zeros((128, 128), jnp.float32)
+    for which, source in enumerate((real[0], imag[0])):
         for spot, origin in enumerate((0, 103, 8, 111)):
-            moved = roll(source, 24 + spot - origin)
-            values = jnp.where(lane == 24 + spot, moved, values)
-        return values
+            at = 4 * which + spot
+            packed = jnp.where(lane == at, roll(source, at - origin), packed)
+    store(out_ref, 24, 25, packed)
 
     state = lambda group, q: (
         block(state_ref, 8 * group + 2 * q),
         block(state_ref, 8 * group + 2 * q + 1),
     )
-    send_fields(tab, rank, state, out_ref, 26, ("u", "v", "wx"), extra)
-
-
-def product_one(tab, in_ref, count, last, place):
+    hidden = block(state_ref, 16), block(state_ref, 17)
+    send_fields(tab, rank, state, hidden, out_ref, 25, ("u", "v", "wx"))
+
+
+def product_one(tab, in_ref, count, edge, place):
     real, imag = load_set(in_ref, 8 * place, count)
-    return y_inverse(tab, real, imag, last, place)
-
-
-def drive_rows(tab, real, imag):
-    lane = lane_ids()
-    columns = jnp.where(lane < 4, roll(real, -24), roll(imag, -20)).T
+    return y_inverse(tab, real, imag, edge, place)
+
+
+def drive_rows(tab, values):
+    columns = values.T
     pick = lambda index: jnp.broadcast_to(columns[index : index + 1, :], (8, 128))
     plus = swap4([pick(4 * part + k) for part in range(2) for k in range(2)])
     minus = swap4([pick(4 * part + 2 + k) for part in range(2) for k in range(2)])
@@ -502,30 +567,25 @@
 def product_first_kernel(in_ref, local_ref, *rest):
     tab = Tables(PRODUCT, rest)
     out_ref = rest[len(PRODUCT)]
-    last_real, last_imag = load(in_ref, 24, 26), load(in_ref, 25, 26)
-    store(out_ref, 16, 17, drive_rows(tab, last_real, last_imag))
-    last = last_row(tab, last_real, last_imag)
-    u0, u1 = product_one(tab, in_ref, 26, last, 0)
-    x0, x1 = product_one(tab, in_ref, 26, last, 2)
-    sum0 = [a * b for a, b in zip(u0, x0)]
-    sum1 = [a * b for a, b in zip(u1, x1)]
+    store(out_ref, 16, 17, drive_rows(tab, load(in_ref, 24, 25)))
     lane = lane_ids()
-    row = 32 * row_ids() + (lane >> 3)
+    upper = (lane < 8) & (row_ids() >= 64)
+    row = 32 * row_ids() + jnp.where(upper, 16, lane >> 3)
     slope = jnp.where(row < GRID // 2, row, row - GRID)
     slope = jnp.where(row == GRID // 2, 0, slope).astype(jnp.float32) * unit
     real, imag = load_set(local_ref, 0, 17)
-    real, imag = [-b * slope for b in imag], [a * slope for a in real]
-    row = 32 * row_ids() + 16
-    slope = jnp.where(row < GRID // 2, row, row - GRID).astype(jnp.float32) * unit
-    last_real, last_imag = 0.0, 0.0
-    for xh in range(4):
-        mine = (lane >> 3) == 4 * xh
-        a, b = load(local_ref, 8 + xh, 17), load(local_ref, 12 + xh, 17)
-        last_real = jnp.where(mine, roll(-b * slope, 32 * xh), last_real)
-        last_imag = jnp.where(mine, roll(a * slope, 32 * xh), last_imag)
-    own = last_row(tab, last_real, last_imag)
-    y0, y1 = y_inverse(tab, real, imag, own, 0)
-    v0, v1 = product_one(tab, in_ref, 26, last, 1)
+    other_real, other_imag = load_set(local_ref, 8, 17)
+    own = (
+        [-slope * jnp.where(upper, b, a) for a, b in zip(imag, other_imag)],
+        [slope * jnp.where(upper, b, a) for a, b in zip(real, other_real)],
+    )
+    last = edge_rows(tab, [load_set(in_ref, 8 * k, 25) for k in range(3)] + [own])
+    u0, u1 = product_one(tab, in_ref, 25, last, 0)
+    x0, x1 = product_one(tab, in_ref, 25, last, 2)
+    sum0 = [a * b for a, b in zip(u0, x0)]
+    sum1 = [a * b for a, b in zip(u1, x1)]
+    y0, y1 = y_inverse(tab, *own, last, 3)
+    v0, v1 = product_one(tab, in_ref, 25, last, 1)
     sum0 = [s + a * b for s, a, b in zip(sum0, v0, y0)]
     sum1 = [s + a * b for s, a, b in zip(sum1, v1, y1)]
     direct, mirror = y_forward(tab, list(zip(sum0, sum1)))
@@ -536,14 +596,14 @@
 def product_kernel(in_ref, *rest):
     tab = Tables(LAST, rest)
     out_ref, mixed_ref = rest[len(LAST) :]
-    got = load(in_ref, 34, 35)
+    got = load(in_ref, 32, 33)
     mixed_ref[0:4, :] = got[0:4, :]
     mixed_ref[4:8, :] = got[124:128, :]
-    last = last_row(tab, load(in_ref, 32, 35), load(in_ref, 33, 35))
+    last = edge_rows(tab, [load_set(in_ref, 8 * k, 33) for k in range(4)])
     sum0, sum1 = None, None
     for one, two in ((0, 2), (1, 3)):
-        a0, a1 = product_one(tab, in_ref, 35, last, one)
-        b0, b1 = product_one(tab, in_ref, 35, last, two)
+        a0, a1 = product_one(tab, in_ref, 33, last, one)
+        b0, b1 = product_one(tab, in_ref, 33, last, two)
         made0 = [a * b for a, b in zip(a0, b0)]
         made1 = [a * b for a, b in zip(a1, b1)]
         sum0 = made0 if sum0 is None else [s + m for s, m in zip(sum0, made0)]
@@ -642,7 +702,8 @@
                 )
                 slope = drive - keep * term - damp * now
                 after = now + time_step * slope
-                put(next_ref, place, after)
+                if place < 10:
+                    put(next_ref, place, after)
                 rest_slope = slope + drive - damp * after
                 change = 0.5 * time_step * rest_slope
                 lifted = now + change + (coarse_ratio * low) * change
@@ -657,12 +718,15 @@
     both = [jnp.where(lane < 32, e, roll(o, 32)) for e, o in zip(even, odd)]
     both = [jnp.where(lane < 64, b, 0.0) for b in both]
     second, first = left_many(tab["left"], [both[1]], [both[0]])
-    store(out_ref, 34, 35, jnp.where(lane < 64, first[0], roll(second[0], 64)))
+    store(out_ref, 32, 33, jnp.where(lane < 64, first[0], roll(second[0], 64)))
     state = lambda group, q: (
         block(next_ref, 8 * group + 2 * q),
         block(next_ref, 8 * group + 2 * q + 1),
     )
-    send_fields(tab, rank, state, out_ref, 35, ("u", "v", "wx", "wy"))
+    damp = (viscosity * unit * unit) * (squares + float((GRID // 2) ** 2))
+    fade = 1.0 - time_step * damp
+    hidden = block(state_ref, 16) * fade, block(state_ref, 17) * fade
+    send_fields(tab, rank, state, hidden, out_ref, 33, ("u", "v", "wx", "wy"))
 
 
 def final_kernel(cutoff_from, in_ref, ahead_ref, mixed_ref, *rest):
@@ -768,9 +832,9 @@
     )
     got = exchange(sent, 17)
     state, fields = call(
-        start_kernel, "start", [spectrum, (128 * 26, 128)], (got,) + tabs(WAVES)
-    )
-    got = exchange(fields, 26)
+        start_kernel, "start", [(18 * 128, 128), (128 * 25, 128)], (got,) + tabs(START)
+    )
+    got = exchange(fields, 25)
     (term,) = call(
         product_first_kernel, "product_first", [(128 * 17, 128)], (got, near(sent)) + tabs(PRODUCT)
     )
@@ -778,17 +842,17 @@
     ahead, fields = call(
         middle_kernel,
         "middle",
-        [spectrum, (128 * 35, 128)],
+        [spectrum, (128 * 33, 128)],
         (got, near(state)) + tabs(MIDDLE),
         (cutoff, forcing_shells),
         scratch=[
-            pltpu.VMEM(spectrum, jnp.float32),
+            pltpu.VMEM((10 * 128, 128), jnp.float32),
             pltpu.SMEM((1,), jnp.int32),
             pltpu.SMEM((SHELLS,), jnp.int32),
             pltpu.SemaphoreType.DMA((2,)),
         ],
     )
-    got = exchange(fields, 35)
+    got = exchange(fields, 33)
     term, mixed = call(
         product_kernel, "product", [(128 * 20, 128), (8, 128)], (got,) + tabs(LAST)
     )

time: 175 us -> 175 us (level)
  blocking collectives: 147 us -> 145 us
    all_to_all x5, blocking collectives: 147 us -> 145 us  [exchange(): cut = lax.all_to_all(cut, AXES, split_axis=0, concat_axis=0, tiled=True)]
where the time goes in v3:
time: 175 us; the launch traced here: 174 us
  blocking collectives  145 us (83%)
  Pallas kernels  27.3 us (16%)
    all_to_all x5, blocking collectives, exchange(): cut = lax.all_to_all(cut, AXES, split_axis=0, concat_axis=0, tiled=True)  145 us
    pallas_call x6, Pallas kernels, call(): pl.pallas_call(kernel, name=name, out_shape=[jax.ShapeDtypeStruct(shape,...  27.3 us

profile of v3, /device:TPU:1, one launch (start us, length us, event | category | flops | bytes accessed | tf_op | source)
XLA Modules:
  0.0 174.3 jit_solution(16541164698648643477)
XLA Ops:
  1.3 3.7 %first.1.local_ref = f32[2176,128]{1,0:T(8,128)S(1)} custom-call(f32[32,4096]{1,0:T(8,128)} %rest_0_.6, f32[32,4096]{1,0:T(8,128)} %rest_1_.6, bf16[256,512]{1,0:T(8,128)(2,1)} %constant.34.clone.rest_2_.rest_0_, bf16[512,256]{1,0:T(8,128)(2,1)} %constant.37.clone.rest_3_.rest_2_, f32[512,128]{1,0:T(8,128)} %constant.40.clone.rest_4_, ...), custom_call_target="tpu_custom_call" | custom-call | tf_op jit(solution)/shard_map/first/pallas_call | solution.py:798
  5.0 0.0 copy-start
  5.0 0.0 copy-start.1
  5.0 0.0 copy-start.4
  5.0 0.0 copy-start.5
  5.0 0.0 copy-start.12
  5.0 31.7 %all_to_all.25 = f32[128,1,2176]{2,1,0:T(1,128)S(1)} all-to-all(f32[128,1,2176]{2,1,0:T(1,128)S(1)} %bitcast.10), channel_id=1, replica_groups=mesh['gx'=32,'gy'=4] {'gx','gy'}, dimensions={0} | all-to-all | bytes 2228224 | tf_op jit(solution)/shard_map/all_to_all | solution.py:815
  36.8 0.0 copy-done
  36.8 0.0 copy-done.1
  36.8 4.2 %start.1 = (f32[2304,128]{1,0:T(8,128)S(1)}, f32[3200,128]{1,0:T(8,128)S(1)}) custom-call(f32[2176,128]{1,0:T(8,128)S(1)} %bitcast.16, bf16[256,512]{1,0:T(8,128)(2,1)S(1)} %copy-done, bf16[512,256]{1,0:T(8,128)(2,1)S(1)} %copy-done.1, f32[256,128]{1,0:T(8,128)S(1)} %copy-done.5, f32[384,128]{1,0:T(8,128)S(1)} %copy-done.4, bf16[384,128]{1,0:T(8,128)(2,1)S(1)} %copy-done.12), custom_call_target="tpu_custom_call" | custom-call | tf_op jit(solution)/shard_map/start/pallas_call | solution.py:798
  41.0 0.0 copy-start.2
  41.0 0.0 copy-start.3
  41.0 0.0 copy-start.6
  41.0 0.0 copy-start.7
  41.0 0.0 copy-start.13
  41.0 29.3 %all_to_all.26 = f32[128,1,3200]{2,1,0:T(1,128)S(1)} all-to-all(f32[128,1,3200]{2,1,0:T(1,128)S(1)} %bitcast.18), channel_id=1, replica_groups=mesh['gx'=32,'gy'=4] {'gx','gy'}, dimensions={0} | all-to-all | bytes 3276800 | tf_op jit(solution)/shard_map/all_to_all | solution.py:815
  70.3 0.0 copy-done.3
  70.3 4.2 %product_first.1 = f32[2176,128]{1,0:T(8,128)S(1)} custom-call(f32[3200,128]{1,0:T(8,128)S(1)} %bitcast.12, f32[2176,128]{1,0:T(8,128)S(1)} %first.1.local_ref, bf16[256,512]{1,0:T(8,128)(2,1)S(1)} %copy-done, bf16[256,512]{1,0:T(8,128)(2,1)S(1)} %copy-done.7, bf16[512,256]{1,0:T(8,128)(2,1)S(1)} %copy-done.3, bf16[512,256]{1,0:T(8,128)(2,1)S(1)} %copy-done.6, ...), custom_call_target="tpu_custom_call" | custom-call | tf_op jit(solution)/shard_map/product_first/pallas_call | solution.py:798
  74.5 0.0 copy-start.11
  74.5 0.0 copy-start.15
  74.5 23.6 %all_to_all.27 = f32[128,1,2176]{2,1,0:T(1,128)S(1)} all-to-all(f32[128,1,2176]{2,1,0:T(1,128)S(1)} %bitcast.14), channel_id=1, replica_groups=mesh['gx'=32,'gy'=4] {'gx','gy'}, dimensions={0} | all-to-all | bytes 2228224 | tf_op jit(solution)/shard_map/all_to_all | solution.py:815
  98.2 0.0 copy-done.15
  98.2 6.4 %middle.1 = (f32[2048,128]{1,0:T(8,128)S(1)}, f32[4224,128]{1,0:T(8,128)S(1)}) custom-call(s32[1]{0:T(128)S(6)} %copy.28.rest_7_.cutoff_from, s32[4]{0:T(128)S(1)} %copy-done.15, f32[2176,128]{1,0:T(8,128)S(1)} %bitcast.15, f32[2304,128]{1,0:T(8,128)S(1)} %get-tuple-element.9.state_ref, bf16[256,512]{1,0:T(8,128)(2,1)S(1)} %copy-done, ...), custom_call_target="tpu_custom_call" | custom-call | tf_op jit(solution)/shard_map/middle/pallas_call | solution.py:798
  104.5 0.0 copy-start.8
  104.6 0.0 copy-start.10
  104.6 34.9 %all_to_all.28 = f32[128,1,4224]{2,1,0:T(1,128)S(1)} all-to-all(f32[128,1,4224]{2,1,0:T(1,128)S(1)} %bitcast.17), channel_id=1, replica_groups=mesh['gx'=32,'gy'=4] {'gx','gy'}, dimensions={0} | all-to-all | bytes 4325376 | tf_op jit(solution)/shard_map/all_to_all | solution.py:815
  139.4 4.8 %product.1 = (f32[2560,128]{1,0:T(8,128)S(1)}, f32[8,128]{1,0:T(8,128)S(1)}) custom-call(f32[4224,128]{1,0:T(8,128)S(1)} %bitcast.11, bf16[256,512]{1,0:T(8,128)(2,1)S(1)} %copy-done, bf16[256,512]{1,0:T(8,128)(2,1)S(1)} %copy-done.7, bf16[512,256]{1,0:T(8,128)(2,1)S(1)} %copy-done.3, bf16[512,256]{1,0:T(8,128)(2,1)S(1)} %copy-done.6, ...), custom_call_target="tpu_custom_call" | custom-call | tf_op jit(solution)/shard_map/product/pallas_call | solution.py:798
  144.3 0.0 copy-start.9
  144.3 0.0 copy-start.14
  144.3 25.7 %all_to_all.29 = f32[128,1,2560]{2,1,0:T(1,128)S(1)} all-to-all(f32[128,1,2560]{2,1,0:T(1,128)S(1)} %bitcast.19), channel_id=1, replica_groups=mesh['gx'=32,'gy'=4] {'gx','gy'}, dimensions={0} | all-to-all | bytes 2621440 | tf_op jit(solution)/shard_map/all_to_all | solution.py:815
  170.0 0.0 copy-done.14
  170.0 4.1 %final.1 = (f32[2,32,4096]{2,1,0:T(8,128)}, f32[2,256]{1,0:T(2,128)}) custom-call(s32[1]{0:T(128)S(6)} %copy.28.rest_7_.cutoff_from, f32[2560,128]{1,0:T(8,128)S(1)} %bitcast.13, f32[2048,128]{1,0:T(8,128)S(1)} %get-tuple-element.12.ahead_ref, f32[8,128]{1,0:T(8,128)S(1)} %get-tuple-element.13.mixed_ref, bf16[256,512]{1,0:T(8,128)(2,1)S(1)} %copy-done, ...), custom_call_target="tpu_custom_call" | custom-call | tf_op jit(solution)/shard_map/final/pallas_call | solution.py:798
  (11 shorter events, 0.0 us)
Async XLA Ops:
  5.0 31.8 %copy-start = (bf16[256,512]{1,0:T(8,128)(2,1)S(1)}, bf16[256,512]{1,0:T(8,128)(2,1)}, u32[]{:S(2)}) copy-start(bf16[256,512]{1,0:T(8,128)(2,1)} %constant.34.clone.rest_2_.rest_0_) | copy-start | bytes 786436
  5.0 31.8 %copy-start.1 = (bf16[512,256]{1,0:T(8,128)(2,1)S(1)}, bf16[512,256]{1,0:T(8,128)(2,1)}, u32[]{:S(2)}) copy-start(bf16[512,256]{1,0:T(8,128)(2,1)} %constant.36.clone.rest_1_) | copy-start | bytes 786436
  5.0 31.8 %copy-start.4 = (f32[384,128]{1,0:T(8,128)S(1)}, f32[384,128]{1,0:T(8,128)}, u32[]{:S(2)}) copy-start(f32[384,128]{1,0:T(8,128)} %constant.42.clone.rest_3_) | copy-start | bytes 589828
  5.0 31.8 %copy-start.5 = (f32[256,128]{1,0:T(8,128)S(1)}, f32[256,128]{1,0:T(8,128)}, u32[]{:S(2)}) copy-start(f32[256,128]{1,0:T(8,128)} %constant.39.clone.rest_2_) | copy-start | bytes 393220
  5.0 31.8 %copy-start.12 = (bf16[384,128]{1,0:T(8,128)(2,1)S(1)}, bf16[384,128]{1,0:T(8,128)(2,1)}, u32[]{:S(2)}) copy-start(bf16[384,128]{1,0:T(8,128)(2,1)} %constant.46.clone.rest_4_) | copy-start | bytes 294916
  41.0 29.3 %copy-start.2 = (f32[512,128]{1,0:T(8,128)S(1)}, f32[512,128]{1,0:T(8,128)}, u32[]{:S(2)}) copy-start(f32[512,128]{1,0:T(8,128)} %constant.40.clone.rest_4_) | copy-start | bytes 786436
  41.0 29.3 %copy-start.3 = (bf16[512,256]{1,0:T(8,128)(2,1)S(1)}, bf16[512,256]{1,0:T(8,128)(2,1)}, u32[]{:S(2)}) copy-start(bf16[512,256]{1,0:T(8,128)(2,1)} %constant.37.clone.rest_3_.rest_2_) | copy-start | bytes 786436
  41.0 29.3 %copy-start.6 = (bf16[512,256]{1,0:T(8,128)(2,1)S(1)}, bf16[512,256]{1,0:T(8,128)(2,1)}, u32[]{:S(2)}) copy-start(bf16[512,256]{1,0:T(8,128)(2,1)} %constant.38.clone.rest_3_) | copy-start | bytes 786436
  41.0 29.3 %copy-start.7 = (bf16[256,512]{1,0:T(8,128)(2,1)S(1)}, bf16[256,512]{1,0:T(8,128)(2,1)}, u32[]{:S(2)}) copy-start(bf16[256,512]{1,0:T(8,128)(2,1)} %constant.35.clone.rest_1_) | copy-start | bytes 786436
  41.0 29.3 %copy-start.13 = (bf16[256,128]{1,0:T(8,128)(2,1)S(1)}, bf16[256,128]{1,0:T(8,128)(2,1)}, u32[]{:S(2)}) copy-start(bf16[256,128]{1,0:T(8,128)(2,1)} %constant.43.clone.rest_5_) | copy-start | bytes 196612
  74.5 23.7 %copy-start.11 = (f32[256,128]{1,0:T(8,128)S(1)}, f32[256,128]{1,0:T(8,128)}, u32[]{:S(2)}) copy-start(f32[256,128]{1,0:T(8,128)} %constant.41.clone.rest_4_) | copy-start | bytes 393220
  74.5 23.6 %copy-start.15 = (s32[4]{0:T(128)S(1)}, s32[4]{0:T(128)}, u32[]{:S(2)}) copy-start(s32[4]{0:T(128)} %shells_from.1) | copy-start | bytes 52
  104.5 34.9 %copy-start.8 = (bf16[1024,256]{1,0:T(8,128)(2,1)S(1)}, bf16[1024,256]{1,0:T(8,128)(2,1)}, u32[]{:S(2)}) copy-start(bf16[1024,256]{1,0:T(8,128)(2,1)} %constant.49.clone.rest_5_) | copy-start | bytes 1572868
  104.6 34.9 %copy-start.10 = (bf16[256,256]{1,0:T(8,128)(2,1)S(1)}, bf16[256,256]{1,0:T(8,128)(2,1)}, u32[]{:S(2)}) copy-start(bf16[256,256]{1,0:T(8,128)(2,1)} %constant.50.clone.rest_6_) | copy-start | bytes 393220
  144.3 25.8 %copy-start.9 = (bf16[256,512]{1,0:T(8,128)(2,1)S(1)}, bf16[256,512]{1,0:T(8,128)(2,1)}, u32[]{:S(2)}) copy-start(bf16[256,512]{1,0:T(8,128)(2,1)} %constant.44.clone.rest_4_) | copy-start | bytes 786436
  144.3 25.8 %copy-start.14 = (f32[16,256]{1,0:T(8,128)S(1)}, f32[16,256]{1,0:T(8,128)}, u32[]{:S(2)}) copy-start(f32[16,256]{1,0:T(8,128)} %constant.45.clone.rest_5_) | copy-start | bytes 49156

commit v4 on v3

--- a/solution.py
+++ b/solution.py
@@ -416,8 +416,9 @@
     high, low = halves(both)
     pair = jnp.concatenate([high, low], axis=1)
     twice = lambda table, axis: jnp.concatenate([table, table], axis=axis)
-    most = dot(pair, twice(flip[:128], 0))
-    top = dot(pair, twice(flip[128:256], 0))
+    lanes = jnp.concatenate([flip[:128], flip[128:256]], axis=1)
+    out = dot(pair, twice(lanes, 0))
+    most, top = out[:, :128], out[:, 128:]
     wide = jnp.concatenate([most[:128], most[128:]], axis=1)
     high, low = halves(wide)
     wide = dot(twice(flip[256:], 1), jnp.concatenate([high, low], axis=0))
@@ -741,26 +742,24 @@
     low_x = tab.turn("wave_x", 2) * coarse_ratio
     copies = []
     for group in range(2):
-        real, imag = spectra[group]
+        factors = []
         for q in range(4):
             rows = Rows(rank, group, q)
             factor = keep_x * rows.keep(cutoff)
-            factor = factor + factor * (low_x * rows.low())
-            for part, term in enumerate((real[q], imag[q])):
-                lifted = block(ahead_ref, 8 * group + 2 * q + part) - factor * term
-                flipped = lifted.T
+            factors.append(factor + factor * (low_x * rows.low()))
+        for part in range(2):
+            for q in range(4):
+                lifted = block(ahead_ref, 8 * group + 2 * q + part)
+                flipped = (lifted - factors[q] * spectra[group][part][q]).T
                 for kh in range(4):
                     for slot in range(4):
                         at = 32 * kh + 8 * slot
-                        piece = flipped[at : at + 8, :]
                         number = 4 * q + slot
                         if group == 1:
                             number = 16 if number == 0 else 32 - number
-                        for kl in range(8):
-                            col = 128 * (8 * kh + kl)
-                            held_ref[part, number, col : col + 128] = piece[kl]
-        for part in range(2):
-            spot = (part, slice(16 * group, 16 * group + 16))
+                        start = 1024 * part + 256 * (number // 8) + 64 * kh + number % 8
+                        held_ref[pl.ds(start, 8, stride=8), :] = flipped[at : at + 8, :]
+            spot = slice(1024 * part + 512 * group, 1024 * part + 512 * group + 512)
             copies.append(
                 pltpu.make_async_copy(
                     held_ref.at[spot], out_ref.at[spot], done_ref.at[2 * group + part]
@@ -860,17 +859,18 @@
     lifted, coarse = call(
         final_kernel,
         "final",
-        [(2, 32, GRID), (2, LOW)],
+        [(2048, 128), (2, LOW)],
         (got, near(ahead), mixed) + tabs(FINAL),
         (cutoff,),
         out_specs=[HBM, VMEM],
         scratch=[
-            pltpu.VMEM((2, 32, GRID), jnp.float32),
+            pltpu.VMEM((2048, 128), jnp.float32),
             pltpu.SMEM((1,), jnp.int32),
             pltpu.SemaphoreType.DMA((1,)),
             pltpu.SemaphoreType.DMA((4,)),
         ],
     )
+    lifted = lifted.reshape(2, 4, 32, 8, 128).transpose(0, 1, 3, 2, 4).reshape(2, 32, GRID)
     return lifted, coarse
 
 

time: 175 us -> 174 us (level)
  no operation moved by 1% of the time
where the time goes in v4:
time: 174 us
  blocking collectives  145 us (83%)
  Pallas kernels  27 us (16%)
    all_to_all x5, blocking collectives, exchange(): cut = lax.all_to_all(cut, AXES, split_axis=0, concat_axis=0, tiled=True)  145 us
    pallas_call x6, Pallas kernels, call(): pl.pallas_call(kernel, name=name, out_shape=[jax.ShapeDtypeStruct(shape,...  27 us

profile of v4, /device:TPU:1, one launch (start us, length us, event | category | flops | bytes accessed | tf_op | source)
XLA Modules:
  0.0 173.9 jit_solution(8509037384967088200)
XLA Ops:
  1.3 3.7 %first.1.local_ref = f32[2176,128]{1,0:T(8,128)S(1)} custom-call(f32[32,4096]{1,0:T(8,128)} %rest_0_.6, f32[32,4096]{1,0:T(8,128)} %rest_1_.6, bf16[256,512]{1,0:T(8,128)(2,1)} %constant.34.clone.rest_2_.rest_0_, bf16[512,256]{1,0:T(8,128)(2,1)} %constant.37.clone.rest_3_.rest_2_, f32[512,128]{1,0:T(8,128)} %constant.40.clone.rest_4_, ...), custom_call_target="tpu_custom_call" | custom-call | tf_op jit(solution)/shard_map/first/pallas_call | solution.py:797
  5.0 0.0 copy-start
  5.0 0.0 copy-start.1
  5.0 0.0 copy-start.4
  5.0 0.0 copy-start.5
  5.0 0.0 copy-start.12
  5.0 31.7 %all_to_all.25 = f32[128,1,2176]{2,1,0:T(1,128)S(1)} all-to-all(f32[128,1,2176]{2,1,0:T(1,128)S(1)} %bitcast.15), channel_id=1, replica_groups=mesh['gx'=32,'gy'=4] {'gx','gy'}, dimensions={0} | all-to-all | bytes 2228224 | tf_op jit(solution)/shard_map/all_to_all | solution.py:814
  36.8 0.0 copy-done
  36.8 4.2 %start.1 = (f32[2304,128]{1,0:T(8,128)S(1)}, f32[3200,128]{1,0:T(8,128)S(1)}) custom-call(f32[2176,128]{1,0:T(8,128)S(1)} %bitcast.21, bf16[256,512]{1,0:T(8,128)(2,1)S(1)} %copy-done, bf16[512,256]{1,0:T(8,128)(2,1)S(1)} %copy-done.1, f32[256,128]{1,0:T(8,128)S(1)} %copy-done.5, f32[384,128]{1,0:T(8,128)S(1)} %copy-done.4, bf16[384,128]{1,0:T(8,128)(2,1)S(1)} %copy-done.12), custom_call_target="tpu_custom_call" | custom-call | tf_op jit(solution)/shard_map/start/pallas_call | solution.py:797
  41.0 0.0 copy-start.2
  41.0 0.0 copy-start.3
  41.0 0.0 copy-start.6
  41.0 0.0 copy-start.7
  41.0 0.0 copy-start.13
  41.1 29.2 %all_to_all.26 = f32[128,1,3200]{2,1,0:T(1,128)S(1)} all-to-all(f32[128,1,3200]{2,1,0:T(1,128)S(1)} %bitcast.23), channel_id=1, replica_groups=mesh['gx'=32,'gy'=4] {'gx','gy'}, dimensions={0} | all-to-all | bytes 3276800 | tf_op jit(solution)/shard_map/all_to_all | solution.py:814
  70.3 0.0 copy-done.2
  70.3 0.0 copy-done.6
  70.3 4.2 %product_first.1 = f32[2176,128]{1,0:T(8,128)S(1)} custom-call(f32[3200,128]{1,0:T(8,128)S(1)} %bitcast.17, f32[2176,128]{1,0:T(8,128)S(1)} %first.1.local_ref, bf16[256,512]{1,0:T(8,128)(2,1)S(1)} %copy-done, bf16[256,512]{1,0:T(8,128)(2,1)S(1)} %copy-done.7, bf16[512,256]{1,0:T(8,128)(2,1)S(1)} %copy-done.3, bf16[512,256]{1,0:T(8,128)(2,1)S(1)} %copy-done.6, ...), custom_call_target="tpu_custom_call" | custom-call | tf_op jit(solution)/shard_map/product_first/pallas_call | solution.py:797
  74.5 0.0 copy-start.11
  74.5 0.0 copy-start.15
  74.5 23.6 %all_to_all.27 = f32[128,1,2176]{2,1,0:T(1,128)S(1)} all-to-all(f32[128,1,2176]{2,1,0:T(1,128)S(1)} %bitcast.19), channel_id=1, replica_groups=mesh['gx'=32,'gy'=4] {'gx','gy'}, dimensions={0} | all-to-all | bytes 2228224 | tf_op jit(solution)/shard_map/all_to_all | solution.py:814
  98.2 6.4 %middle.1 = (f32[2048,128]{1,0:T(8,128)S(1)}, f32[4224,128]{1,0:T(8,128)S(1)}) custom-call(s32[1]{0:T(128)S(6)} %copy.28.rest_7_.cutoff_from, s32[4]{0:T(128)S(1)} %copy-done.15, f32[2176,128]{1,0:T(8,128)S(1)} %bitcast.20, f32[2304,128]{1,0:T(8,128)S(1)} %get-tuple-element.11.state_ref, bf16[256,512]{1,0:T(8,128)(2,1)S(1)} %copy-done, ...), custom_call_target="tpu_custom_call" | custom-call | tf_op jit(solution)/shard_map/middle/pallas_call | solution.py:797
  104.6 0.0 copy-start.8
  104.6 0.0 copy-start.10
  104.6 34.9 %all_to_all.28 = f32[128,1,4224]{2,1,0:T(1,128)S(1)} all-to-all(f32[128,1,4224]{2,1,0:T(1,128)S(1)} %bitcast.22), channel_id=1, replica_groups=mesh['gx'=32,'gy'=4] {'gx','gy'}, dimensions={0} | all-to-all | bytes 4325376 | tf_op jit(solution)/shard_map/all_to_all | solution.py:814
  139.5 0.0 copy-done.8
  139.5 4.8 %product.1 = (f32[2560,128]{1,0:T(8,128)S(1)}, f32[8,128]{1,0:T(8,128)S(1)}) custom-call(f32[4224,128]{1,0:T(8,128)S(1)} %bitcast.16, bf16[256,512]{1,0:T(8,128)(2,1)S(1)} %copy-done, bf16[256,512]{1,0:T(8,128)(2,1)S(1)} %copy-done.7, bf16[512,256]{1,0:T(8,128)(2,1)S(1)} %copy-done.3, bf16[512,256]{1,0:T(8,128)(2,1)S(1)} %copy-done.6, ...), custom_call_target="tpu_custom_call" | custom-call | tf_op jit(solution)/shard_map/product/pallas_call | solution.py:797
  144.3 0.0 copy-start.9
  144.3 0.0 copy-start.14
  144.3 25.7 %all_to_all.29 = f32[128,1,2560]{2,1,0:T(1,128)S(1)} all-to-all(f32[128,1,2560]{2,1,0:T(1,128)S(1)} %bitcast.24), channel_id=1, replica_groups=mesh['gx'=32,'gy'=4] {'gx','gy'}, dimensions={0} | all-to-all | bytes 2621440 | tf_op jit(solution)/shard_map/all_to_all | solution.py:814
  170.0 0.0 copy-done.14
  170.0 3.7 %final.1 = (f32[2048,128]{1,0:T(8,128)}, f32[2,256]{1,0:T(2,128)}) custom-call(s32[1]{0:T(128)S(6)} %copy.28.rest_7_.cutoff_from, f32[2560,128]{1,0:T(8,128)S(1)} %bitcast.18, f32[2048,128]{1,0:T(8,128)S(1)} %get-tuple-element.14.ahead_ref, f32[8,128]{1,0:T(8,128)S(1)} %get-tuple-element.15.mixed_ref, bf16[256,512]{1,0:T(8,128)(2,1)S(1)} %copy-done, ...), custom_call_target="tpu_custom_call" | custom-call | tf_op jit(solution)/shard_map/final/pallas_call | solution.py:797
  (11 shorter events, 0.0 us)
Async XLA Ops:
  5.0 31.8 %copy-start = (bf16[256,512]{1,0:T(8,128)(2,1)S(1)}, bf16[256,512]{1,0:T(8,128)(2,1)}, u32[]{:S(2)}) copy-start(bf16[256,512]{1,0:T(8,128)(2,1)} %constant.34.clone.rest_2_.rest_0_) | copy-start | bytes 786436
  5.0 31.8 %copy-start.1 = (bf16[512,256]{1,0:T(8,128)(2,1)S(1)}, bf16[512,256]{1,0:T(8,128)(2,1)}, u32[]{:S(2)}) copy-start(bf16[512,256]{1,0:T(8,128)(2,1)} %constant.36.clone.rest_1_) | copy-start | bytes 786436
  5.0 31.8 %copy-start.4 = (f32[384,128]{1,0:T(8,128)S(1)}, f32[384,128]{1,0:T(8,128)}, u32[]{:S(2)}) copy-start(f32[384,128]{1,0:T(8,128)} %constant.42.clone.rest_3_) | copy-start | bytes 589828
  5.0 31.8 %copy-start.5 = (f32[256,128]{1,0:T(8,128)S(1)}, f32[256,128]{1,0:T(8,128)}, u32[]{:S(2)}) copy-start(f32[256,128]{1,0:T(8,128)} %constant.39.clone.rest_2_) | copy-start | bytes 393220
  5.0 31.8 %copy-start.12 = (bf16[384,128]{1,0:T(8,128)(2,1)S(1)}, bf16[384,128]{1,0:T(8,128)(2,1)}, u32[]{:S(2)}) copy-start(bf16[384,128]{1,0:T(8,128)(2,1)} %constant.46.clone.rest_4_) | copy-start | bytes 294916
  41.0 29.3 %copy-start.2 = (f32[512,128]{1,0:T(8,128)S(1)}, f32[512,128]{1,0:T(8,128)}, u32[]{:S(2)}) copy-start(f32[512,128]{1,0:T(8,128)} %constant.40.clone.rest_4_) | copy-start | bytes 786436
  41.0 29.3 %copy-start.3 = (bf16[512,256]{1,0:T(8,128)(2,1)S(1)}, bf16[512,256]{1,0:T(8,128)(2,1)}, u32[]{:S(2)}) copy-start(bf16[512,256]{1,0:T(8,128)(2,1)} %constant.37.clone.rest_3_.rest_2_) | copy-start | bytes 786436
  41.0 29.3 %copy-start.6 = (bf16[512,256]{1,0:T(8,128)(2,1)S(1)}, bf16[512,256]{1,0:T(8,128)(2,1)}, u32[]{:S(2)}) copy-start(bf16[512,256]{1,0:T(8,128)(2,1)} %constant.38.clone.rest_3_) | copy-start | bytes 786436
  41.0 29.3 %copy-start.7 = (bf16[256,512]{1,0:T(8,128)(2,1)S(1)}, bf16[256,512]{1,0:T(8,128)(2,1)}, u32[]{:S(2)}) copy-start(bf16[256,512]{1,0:T(8,128)(2,1)} %constant.35.clone.rest_1_) | copy-start | bytes 786436
  41.0 29.3 %copy-start.13 = (bf16[256,128]{1,0:T(8,128)(2,1)S(1)}, bf16[256,128]{1,0:T(8,128)(2,1)}, u32[]{:S(2)}) copy-start(bf16[256,128]{1,0:T(8,128)(2,1)} %constant.43.clone.rest_5_) | copy-start | bytes 196612
  74.5 23.7 %copy-start.11 = (f32[256,128]{1,0:T(8,128)S(1)}, f32[256,128]{1,0:T(8,128)}, u32[]{:S(2)}) copy-start(f32[256,128]{1,0:T(8,128)} %constant.41.clone.rest_4_) | copy-start | bytes 393220
  74.5 23.6 %copy-start.15 = (s32[4]{0:T(128)S(1)}, s32[4]{0:T(128)}, u32[]{:S(2)}) copy-start(s32[4]{0:T(128)} %shells_from.1) | copy-start | bytes 52
  104.6 34.9 %copy-start.8 = (bf16[1024,256]{1,0:T(8,128)(2,1)S(1)}, bf16[1024,256]{1,0:T(8,128)(2,1)}, u32[]{:S(2)}) copy-start(bf16[1024,256]{1,0:T(8,128)(2,1)} %constant.49.clone.rest_5_) | copy-start | bytes 1572868
  104.6 34.9 %copy-start.10 = (bf16[256,256]{1,0:T(8,128)(2,1)S(1)}, bf16[256,256]{1,0:T(8,128)(2,1)}, u32[]{:S(2)}) copy-start(bf16[256,256]{1,0:T(8,128)(2,1)} %constant.50.clone.rest_6_) | copy-start | bytes 393220
  144.3 25.8 %copy-start.9 = (bf16[256,512]{1,0:T(8,128)(2,1)S(1)}, bf16[256,512]{1,0:T(8,128)(2,1)}, u32[]{:S(2)}) copy-start(bf16[256,512]{1,0:T(8,128)(2,1)} %constant.44.clone.rest_4_) | copy-start | bytes 786436
  144.3 25.8 %copy-start.14 = (f32[16,256]{1,0:T(8,128)S(1)}, f32[16,256]{1,0:T(8,128)}, u32[]{:S(2)}) copy-start(f32[16,256]{1,0:T(8,128)} %constant.45.clone.rest_5_) | copy-start | bytes 49156
